TPU v7x, 32 devices: a whole 2x2x4 slice. The times are simulated.
32 devices in a mesh: rep: 2 (over x), shard: 16 (over z, y, core).
Axes of the slice: x: 2, y: 2, z: 4, core: 2. Of those that a mesh axis runs over, the one named last changes fastest.
Arguments:
- ratings_a: float32 [2048, 16384], P(('rep', 'shard')), parts along dimension 0
- mask_a: int32 [2048, 16384], P(('rep', 'shard')), parts along dimension 0
- users_a: float32 [2048, 32], P(('rep', 'shard')), parts along dimension 0
- items_a: float32 [32768, 32], P(('rep', 'shard')), parts along dimension 0
- ratings_b: float32 [2048, 16384], P(('rep', 'shard')), parts along dimension 0
- mask_b: int32 [2048, 16384], P(('rep', 'shard')), parts along dimension 0
- users_b: float32 [2048, 32], P(('rep', 'shard')), parts along dimension 0
- items_b: float32 [32768, 32], P(('rep', 'shard')), parts along dimension 0
Outputs:
- output 1: float32 [2048, 32], P(('rep', 'shard')), parts along dimension 0
- output 2: float32 [32768, 32], P(('rep', 'shard')), parts along dimension 0
- output 3: float32 [2048, 32], P(('rep', 'shard')), parts along dimension 0
- output 4: float32 [32768, 32], P(('rep', 'shard')), parts along dimension 0
There are 2 independent parts. A program takes and returns all parts, laid end to end along the dimension named above; each array names one.
All inputs are finite; a program needn't handle non-finite values.
Results may differ from a plain program's by a relative error of at most 0.00331626.
Values are sent between devices in bfloat16 or wider.
A program may use at most 1 GiB of HBM per device.

v0:
```python
import math
import jax
import jax.numpy as jnp
from jax import lax
from jax.sharding import PartitionSpec as P

SWEEP_STEPS = 4
EPOCHS = 2
WEIGHT_DECAY = 0.05


def local_step(user_cur, item_cur, rate_now, flag_now, step_u, step_v):
    user_low = user_cur.astype(jnp.bfloat16)
    item_low = item_cur.astype(jnp.bfloat16)
    approx = lax.dot_general(user_low, item_low, (((1,), (1,)), ((), ())), preferred_element_type=jnp.float32)
    err_low = (flag_now * (approx - rate_now)).astype(jnp.bfloat16)
    grad_u = jnp.dot(err_low, item_low, preferred_element_type=jnp.float32) + WEIGHT_DECAY * user_cur
    grad_v = lax.dot_general(err_low, user_low, (((0,), (0,)), ((), ())), preferred_element_type=jnp.float32) + WEIGHT_DECAY * item_cur
    return user_cur - step_u * grad_u, item_cur - step_v * grad_v


def solution(mesh):
    shard_count = mesh.shape["shard"]
    row_spec = P(("rep", "shard"), None)
    send_perm = [(source, (source - 1) % shard_count) for source in range(shard_count)]

    def device_body(ratings_a, mask_a, users_a, items_a, ratings_b, mask_b, users_b, items_b):
        users_dev, rank_dim = users_a.shape
        item_blk = items_a.shape[0]
        step_u = 0.5 * math.sqrt(rank_dim) / (item_blk + 2 * rank_dim)
        step_v = 0.5 * math.sqrt(rank_dim) / (users_dev + 2 * rank_dim)
        my_pos = lax.axis_index("shard")
        flags_a = mask_a.astype(jnp.bfloat16)
        flags_b = mask_b.astype(jnp.bfloat16)

        def hop_body(hop_index, carry_state):
            user_a, item_a, user_b, item_b = carry_state
            col_start = ((my_pos + hop_index) % shard_count) * item_blk
            rate_now_a = lax.dynamic_slice_in_dim(ratings_a, col_start, item_blk, axis=1)
            flag_now_a = lax.dynamic_slice_in_dim(flags_a, col_start, item_blk, axis=1)
            rate_now_b = lax.dynamic_slice_in_dim(ratings_b, col_start, item_blk, axis=1)
            flag_now_b = lax.dynamic_slice_in_dim(flags_b, col_start, item_blk, axis=1)

            def one_step(unused, inner_state):
                user_a, item_a, user_b, item_b = inner_state
                user_a, item_a = local_step(user_a, item_a, rate_now_a, flag_now_a, step_u, step_v)
                user_b, item_b = local_step(user_b, item_b, rate_now_b, flag_now_b, step_u, step_v)
                return user_a, item_a, user_b, item_b

            user_a, item_a, user_b, item_b = lax.fori_loop(0, SWEEP_STEPS, one_step, (user_a, item_a, user_b, item_b))
            item_a = lax.ppermute(item_a, "shard", send_perm)
            item_b = lax.ppermute(item_b, "shard", send_perm)
            return user_a, item_a, user_b, item_b

        return lax.fori_loop(0, EPOCHS * shard_count, hop_body, (users_a, items_a, users_b, items_b))

    return jax.shard_map(device_body, mesh=mesh, in_specs=(row_spec,) * 8, out_specs=(row_spec,) * 4, check_vma=False)
```

profile of v0, /device:TPU:0, one launch (start us, length us, event | category | flops | bytes accessed | tf_op | source)
XLA Modules:
  0.0 496.2 jit_solution(14541339331457306894)
XLA Ops:
  5.7 489.9 %while.70 = (s32[]{:T(128)}, f32[64,32]{0,1:T(8,128)S(1)}, f32[1024,32]{0,1:T(8,128)S(1)}, f32[64,32]{0,1:T(8,128)S(1)}, f32[1024,32]{0,1:T(8,128)S(1)}, /*index...) while((s32[]{:T(128)}, f32[64,32]{0,1:T(8,128)S(1)}, ...), condition=%wide.region_3.4_spmd, body=%wide.region_0.3_spmd.sunk | while | flops 26107920 | bytes 5866073 | solution.py:55
  7.7 4.7 while.71
  12.4 5.6 %collective-permute-start.1 = (f32[1024,32]{0,1:T(8,128)S(1)}, f32[1024,32]{0,1:T(8,128)S(1)}, u32[]{:S(2)}, u32[]{:S(2)}) collective-permute-start(f32[1024,32]{0,1:T(8,128)S(1)} %get-tuple-element.496), channel_id=1, source_target_pairs={{0,15},{1,0},{2,1},{3,2},{4,3},{5,4},{6,5},{7,6},{8,7},{9,8},{10,9... | collective-permute-start | bytes 393224 | tf_op jit(solution)/shard_map/while/body/eval_jaxpr/ppermute | solution.py:52
  23.9 4.7 while.71
  28.5 4.7 collective-permute-start.1
  39.2 4.7 while.71
  43.8 4.7 collective-permute-start.1
  54.5 4.7 while.71
  69.7 4.7 while.71
  74.4 4.7 collective-permute-start.1
  85.0 4.7 while.71
  89.7 4.7 collective-permute-start.1
  100.3 4.7 while.71
  105.0 4.7 collective-permute-start.1
  115.6 4.7 while.71
  120.2 4.7 collective-permute-start.1
  130.9 4.7 while.71
  135.5 4.7 collective-permute-start.1
  146.1 4.7 while.71
  150.8 4.7 collective-permute-start.1
  161.4 4.7 while.71
  166.1 4.7 collective-permute-start.1
  176.7 4.7 while.71
  181.4 4.7 collective-permute-start.1
  192.0 4.7 while.71
  196.6 4.7 collective-permute-start.1
  207.3 4.7 while.71
  211.9 4.7 collective-permute-start.1
  222.5 4.7 while.71
  227.2 4.7 collective-permute-start.1
  237.8 4.7 while.71
  242.5 4.7 collective-permute-start.1
  253.1 4.7 while.71
  257.8 4.7 collective-permute-start.1
  268.4 4.7 while.71
  273.0 4.7 collective-permute-start.1
  283.7 4.7 while.71
  288.3 4.7 collective-permute-start.1
  298.9 4.7 while.71
  303.6 4.7 collective-permute-start.1
  314.2 4.7 while.71
  318.9 4.7 collective-permute-start.1
  329.5 4.7 while.71
  334.2 4.7 collective-permute-start.1
  344.8 4.7 while.71
  349.5 4.7 collective-permute-start.1
  360.1 4.7 while.71
  364.7 4.7 collective-permute-start.1
  375.3 4.7 while.71
  380.0 4.7 collective-permute-start.1
  390.6 4.7 while.71
  395.3 4.7 collective-permute-start.1
  405.9 4.7 while.71
  410.6 4.7 collective-permute-start.1
  421.2 4.7 while.71
  425.9 4.7 collective-permute-start.1
  436.5 4.7 while.71
  441.1 4.7 collective-permute-start.1
  451.7 4.7 while.71
  456.4 4.7 collective-permute-start.1
  467.0 4.7 while.71
  471.7 4.7 collective-permute-start.1
  482.3 4.7 while.71
  487.0 4.7 collective-permute-start.1
  (1269 shorter events, 338.2 us)
Async XLA Ops:
  12.4 8.1 %collective-permute-start.1 = (f32[1024,32]{0,1:T(8,128)S(1)}, f32[1024,32]{0,1:T(8,128)S(1)}, u32[]{:S(2)}, u32[]{:S(2)}) collective-permute-start(f32[1024,32]{0,1:T(8,128)S(1)} %get-tuple-element.496), channel_id=1, source_target_pairs={{0,15},{1,0},{2,1},{3,2},{4,3},{5,4},{6,5},{7,6},{8,7},{9,8},{10,9... | collective-permute-start | bytes 393224 | tf_op jit(solution)/shard_map/while/body/eval_jaxpr/ppermute | solution.py:52
  17.9 3.9 collective-permute-start
  28.5 7.2 %collective-permute-start.1 = (f32[1024,32]{0,1:T(8,128)S(1)}, f32[1024,32]{0,1:T(8,128)S(1)}, u32[]{:S(2)}, u32[]{:S(2)}) collective-permute-start(f32[1024,32]{0,1:T(8,128)S(1)} %get-tuple-element.496), channel_id=1, source_target_pairs={{0,15},{1,0},{2,1},{3,2},{4,3},{5,4},{6,5},{7,6},{8,7},{9,8},{10,9... | collective-permute-start | bytes 393224 | tf_op jit(solution)/shard_map/while/body/eval_jaxpr/ppermute | solution.py:52
  33.2 3.9 collective-permute-start
  43.8 7.2 %collective-permute-start.1 = (f32[1024,32]{0,1:T(8,128)S(1)}, f32[1024,32]{0,1:T(8,128)S(1)}, u32[]{:S(2)}, u32[]{:S(2)}) collective-permute-start(f32[1024,32]{0,1:T(8,128)S(1)} %get-tuple-element.496), channel_id=1, source_target_pairs={{0,15},{1,0},{2,1},{3,2},{4,3},{5,4},{6,5},{7,6},{8,7},{9,8},{10,9... | collective-permute-start | bytes 393224 | tf_op jit(solution)/shard_map/while/body/eval_jaxpr/ppermute | solution.py:52
  48.5 3.9 collective-permute-start
  59.1 7.2 %collective-permute-start.1 = (f32[1024,32]{0,1:T(8,128)S(1)}, f32[1024,32]{0,1:T(8,128)S(1)}, u32[]{:S(2)}, u32[]{:S(2)}) collective-permute-start(f32[1024,32]{0,1:T(8,128)S(1)} %get-tuple-element.496), channel_id=1, source_target_pairs={{0,15},{1,0},{2,1},{3,2},{4,3},{5,4},{6,5},{7,6},{8,7},{9,8},{10,9... | collective-permute-start | bytes 393224 | tf_op jit(solution)/shard_map/while/body/eval_jaxpr/ppermute | solution.py:52
  63.8 3.9 collective-permute-start
  74.4 7.2 %collective-permute-start.1 = (f32[1024,32]{0,1:T(8,128)S(1)}, f32[1024,32]{0,1:T(8,128)S(1)}, u32[]{:S(2)}, u32[]{:S(2)}) collective-permute-start(f32[1024,32]{0,1:T(8,128)S(1)} %get-tuple-element.496), channel_id=1, source_target_pairs={{0,15},{1,0},{2,1},{3,2},{4,3},{5,4},{6,5},{7,6},{8,7},{9,8},{10,9... | collective-permute-start | bytes 393224 | tf_op jit(solution)/shard_map/while/body/eval_jaxpr/ppermute | solution.py:52
  79.1 3.9 collective-permute-start
  89.7 7.2 %collective-permute-start.1 = (f32[1024,32]{0,1:T(8,128)S(1)}, f32[1024,32]{0,1:T(8,128)S(1)}, u32[]{:S(2)}, u32[]{:S(2)}) collective-permute-start(f32[1024,32]{0,1:T(8,128)S(1)} %get-tuple-element.496), channel_id=1, source_target_pairs={{0,15},{1,0},{2,1},{3,2},{4,3},{5,4},{6,5},{7,6},{8,7},{9,8},{10,9... | collective-permute-start | bytes 393224 | tf_op jit(solution)/shard_map/while/body/eval_jaxpr/ppermute | solution.py:52
  94.4 3.9 collective-permute-start
  105.0 7.2 %collective-permute-start.1 = (f32[1024,32]{0,1:T(8,128)S(1)}, f32[1024,32]{0,1:T(8,128)S(1)}, u32[]{:S(2)}, u32[]{:S(2)}) collective-permute-start(f32[1024,32]{0,1:T(8,128)S(1)} %get-tuple-element.496), channel_id=1, source_target_pairs={{0,15},{1,0},{2,1},{3,2},{4,3},{5,4},{6,5},{7,6},{8,7},{9,8},{10,9... | collective-permute-start | bytes 393224 | tf_op jit(solution)/shard_map/while/body/eval_jaxpr/ppermute | solution.py:52
  109.6 3.9 collective-permute-start
  120.2 7.2 %collective-permute-start.1 = (f32[1024,32]{0,1:T(8,128)S(1)}, f32[1024,32]{0,1:T(8,128)S(1)}, u32[]{:S(2)}, u32[]{:S(2)}) collective-permute-start(f32[1024,32]{0,1:T(8,128)S(1)} %get-tuple-element.496), channel_id=1, source_target_pairs={{0,15},{1,0},{2,1},{3,2},{4,3},{5,4},{6,5},{7,6},{8,7},{9,8},{10,9... | collective-permute-start | bytes 393224 | tf_op jit(solution)/shard_map/while/body/eval_jaxpr/ppermute | solution.py:52
  124.9 3.9 collective-permute-start
  135.5 7.2 %collective-permute-start.1 = (f32[1024,32]{0,1:T(8,128)S(1)}, f32[1024,32]{0,1:T(8,128)S(1)}, u32[]{:S(2)}, u32[]{:S(2)}) collective-permute-start(f32[1024,32]{0,1:T(8,128)S(1)} %get-tuple-element.496), channel_id=1, source_target_pairs={{0,15},{1,0},{2,1},{3,2},{4,3},{5,4},{6,5},{7,6},{8,7},{9,8},{10,9... | collective-permute-start | bytes 393224 | tf_op jit(solution)/shard_map/while/body/eval_jaxpr/ppermute | solution.py:52
  140.2 3.9 collective-permute-start
  150.8 7.2 %collective-permute-start.1 = (f32[1024,32]{0,1:T(8,128)S(1)}, f32[1024,32]{0,1:T(8,128)S(1)}, u32[]{:S(2)}, u32[]{:S(2)}) collective-permute-start(f32[1024,32]{0,1:T(8,128)S(1)} %get-tuple-element.496), channel_id=1, source_target_pairs={{0,15},{1,0},{2,1},{3,2},{4,3},{5,4},{6,5},{7,6},{8,7},{9,8},{10,9... | collective-permute-start | bytes 393224 | tf_op jit(solution)/shard_map/while/body/eval_jaxpr/ppermute | solution.py:52
  155.5 3.9 collective-permute-start
  166.1 7.2 %collective-permute-start.1 = (f32[1024,32]{0,1:T(8,128)S(1)}, f32[1024,32]{0,1:T(8,128)S(1)}, u32[]{:S(2)}, u32[]{:S(2)}) collective-permute-start(f32[1024,32]{0,1:T(8,128)S(1)} %get-tuple-element.496), channel_id=1, source_target_pairs={{0,15},{1,0},{2,1},{3,2},{4,3},{5,4},{6,5},{7,6},{8,7},{9,8},{10,9... | collective-permute-start | bytes 393224 | tf_op jit(solution)/shard_map/while/body/eval_jaxpr/ppermute | solution.py:52
  170.8 3.9 collective-permute-start
  181.4 7.2 %collective-permute-start.1 = (f32[1024,32]{0,1:T(8,128)S(1)}, f32[1024,32]{0,1:T(8,128)S(1)}, u32[]{:S(2)}, u32[]{:S(2)}) collective-permute-start(f32[1024,32]{0,1:T(8,128)S(1)} %get-tuple-element.496), channel_id=1, source_target_pairs={{0,15},{1,0},{2,1},{3,2},{4,3},{5,4},{6,5},{7,6},{8,7},{9,8},{10,9... | collective-permute-start | bytes 393224 | tf_op jit(solution)/shard_map/while/body/eval_jaxpr/ppermute | solution.py:52
  186.0 3.9 collective-permute-start
  196.6 7.2 %collective-permute-start.1 = (f32[1024,32]{0,1:T(8,128)S(1)}, f32[1024,32]{0,1:T(8,128)S(1)}, u32[]{:S(2)}, u32[]{:S(2)}) collective-permute-start(f32[1024,32]{0,1:T(8,128)S(1)} %get-tuple-element.496), channel_id=1, source_target_pairs={{0,15},{1,0},{2,1},{3,2},{4,3},{5,4},{6,5},{7,6},{8,7},{9,8},{10,9... | collective-permute-start | bytes 393224 | tf_op jit(solution)/shard_map/while/body/eval_jaxpr/ppermute | solution.py:52
  201.3 3.9 collective-permute-start
  211.9 7.2 %collective-permute-start.1 = (f32[1024,32]{0,1:T(8,128)S(1)}, f32[1024,32]{0,1:T(8,128)S(1)}, u32[]{:S(2)}, u32[]{:S(2)}) collective-permute-start(f32[1024,32]{0,1:T(8,128)S(1)} %get-tuple-element.496), channel_id=1, source_target_pairs={{0,15},{1,0},{2,1},{3,2},{4,3},{5,4},{6,5},{7,6},{8,7},{9,8},{10,9... | collective-permute-start | bytes 393224 | tf_op jit(solution)/shard_map/while/body/eval_jaxpr/ppermute | solution.py:52
  216.6 3.9 collective-permute-start
  227.2 7.2 %collective-permute-start.1 = (f32[1024,32]{0,1:T(8,128)S(1)}, f32[1024,32]{0,1:T(8,128)S(1)}, u32[]{:S(2)}, u32[]{:S(2)}) collective-permute-start(f32[1024,32]{0,1:T(8,128)S(1)} %get-tuple-element.496), channel_id=1, source_target_pairs={{0,15},{1,0},{2,1},{3,2},{4,3},{5,4},{6,5},{7,6},{8,7},{9,8},{10,9... | collective-permute-start | bytes 393224 | tf_op jit(solution)/shard_map/while/body/eval_jaxpr/ppermute | solution.py:52
  231.9 3.9 collective-permute-start
  242.5 7.2 %collective-permute-start.1 = (f32[1024,32]{0,1:T(8,128)S(1)}, f32[1024,32]{0,1:T(8,128)S(1)}, u32[]{:S(2)}, u32[]{:S(2)}) collective-permute-start(f32[1024,32]{0,1:T(8,128)S(1)} %get-tuple-element.496), channel_id=1, source_target_pairs={{0,15},{1,0},{2,1},{3,2},{4,3},{5,4},{6,5},{7,6},{8,7},{9,8},{10,9... | collective-permute-start | bytes 393224 | tf_op jit(solution)/shard_map/while/body/eval_jaxpr/ppermute | solution.py:52
  247.2 3.9 collective-permute-start
  257.8 7.2 %collective-permute-start.1 = (f32[1024,32]{0,1:T(8,128)S(1)}, f32[1024,32]{0,1:T(8,128)S(1)}, u32[]{:S(2)}, u32[]{:S(2)}) collective-permute-start(f32[1024,32]{0,1:T(8,128)S(1)} %get-tuple-element.496), channel_id=1, source_target_pairs={{0,15},{1,0},{2,1},{3,2},{4,3},{5,4},{6,5},{7,6},{8,7},{9,8},{10,9... | collective-permute-start | bytes 393224 | tf_op jit(solution)/shard_map/while/body/eval_jaxpr/ppermute | solution.py:52
  262.4 3.9 collective-permute-start
  273.0 7.2 %collective-permute-start.1 = (f32[1024,32]{0,1:T(8,128)S(1)}, f32[1024,32]{0,1:T(8,128)S(1)}, u32[]{:S(2)}, u32[]{:S(2)}) collective-permute-start(f32[1024,32]{0,1:T(8,128)S(1)} %get-tuple-element.496), channel_id=1, source_target_pairs={{0,15},{1,0},{2,1},{3,2},{4,3},{5,4},{6,5},{7,6},{8,7},{9,8},{10,9... | collective-permute-start | bytes 393224 | tf_op jit(solution)/shard_map/while/body/eval_jaxpr/ppermute | solution.py:52
  277.7 3.9 collective-permute-start
  288.3 7.2 %collective-permute-start.1 = (f32[1024,32]{0,1:T(8,128)S(1)}, f32[1024,32]{0,1:T(8,128)S(1)}, u32[]{:S(2)}, u32[]{:S(2)}) collective-permute-start(f32[1024,32]{0,1:T(8,128)S(1)} %get-tuple-element.496), channel_id=1, source_target_pairs={{0,15},{1,0},{2,1},{3,2},{4,3},{5,4},{6,5},{7,6},{8,7},{9,8},{10,9... | collective-permute-start | bytes 393224 | tf_op jit(solution)/shard_map/while/body/eval_jaxpr/ppermute | solution.py:52
  293.0 3.9 collective-permute-start
  303.6 7.2 %collective-permute-start.1 = (f32[1024,32]{0,1:T(8,128)S(1)}, f32[1024,32]{0,1:T(8,128)S(1)}, u32[]{:S(2)}, u32[]{:S(2)}) collective-permute-start(f32[1024,32]{0,1:T(8,128)S(1)} %get-tuple-element.496), channel_id=1, source_target_pairs={{0,15},{1,0},{2,1},{3,2},{4,3},{5,4},{6,5},{7,6},{8,7},{9,8},{10,9... | collective-permute-start | bytes 393224 | tf_op jit(solution)/shard_map/while/body/eval_jaxpr/ppermute | solution.py:52
  308.3 3.9 collective-permute-start
  318.9 7.2 %collective-permute-start.1 = (f32[1024,32]{0,1:T(8,128)S(1)}, f32[1024,32]{0,1:T(8,128)S(1)}, u32[]{:S(2)}, u32[]{:S(2)}) collective-permute-start(f32[1024,32]{0,1:T(8,128)S(1)} %get-tuple-element.496), channel_id=1, source_target_pairs={{0,15},{1,0},{2,1},{3,2},{4,3},{5,4},{6,5},{7,6},{8,7},{9,8},{10,9... | collective-permute-start | bytes 393224 | tf_op jit(solution)/shard_map/while/body/eval_jaxpr/ppermute | solution.py:52
  323.6 3.9 collective-permute-start
  334.2 7.2 %collective-permute-start.1 = (f32[1024,32]{0,1:T(8,128)S(1)}, f32[1024,32]{0,1:T(8,128)S(1)}, u32[]{:S(2)}, u32[]{:S(2)}) collective-permute-start(f32[1024,32]{0,1:T(8,128)S(1)} %get-tuple-element.496), channel_id=1, source_target_pairs={{0,15},{1,0},{2,1},{3,2},{4,3},{5,4},{6,5},{7,6},{8,7},{9,8},{10,9... | collective-permute-start | bytes 393224 | tf_op jit(solution)/shard_map/while/body/eval_jaxpr/ppermute | solution.py:52
  338.9 3.9 collective-permute-start
  349.5 7.2 %collective-permute-start.1 = (f32[1024,32]{0,1:T(8,128)S(1)}, f32[1024,32]{0,1:T(8,128)S(1)}, u32[]{:S(2)}, u32[]{:S(2)}) collective-permute-start(f32[1024,32]{0,1:T(8,128)S(1)} %get-tuple-element.496), channel_id=1, source_target_pairs={{0,15},{1,0},{2,1},{3,2},{4,3},{5,4},{6,5},{7,6},{8,7},{9,8},{10,9... | collective-permute-start | bytes 393224 | tf_op jit(solution)/shard_map/while/body/eval_jaxpr/ppermute | solution.py:52
  354.1 3.9 collective-permute-start
  364.7 7.2 %collective-permute-start.1 = (f32[1024,32]{0,1:T(8,128)S(1)}, f32[1024,32]{0,1:T(8,128)S(1)}, u32[]{:S(2)}, u32[]{:S(2)}) collective-permute-start(f32[1024,32]{0,1:T(8,128)S(1)} %get-tuple-element.496), channel_id=1, source_target_pairs={{0,15},{1,0},{2,1},{3,2},{4,3},{5,4},{6,5},{7,6},{8,7},{9,8},{10,9... | collective-permute-start | bytes 393224 | tf_op jit(solution)/shard_map/while/body/eval_jaxpr/ppermute | solution.py:52
  369.4 3.9 collective-permute-start
  380.0 7.2 %collective-permute-start.1 = (f32[1024,32]{0,1:T(8,128)S(1)}, f32[1024,32]{0,1:T(8,128)S(1)}, u32[]{:S(2)}, u32[]{:S(2)}) collective-permute-start(f32[1024,32]{0,1:T(8,128)S(1)} %get-tuple-element.496), channel_id=1, source_target_pairs={{0,15},{1,0},{2,1},{3,2},{4,3},{5,4},{6,5},{7,6},{8,7},{9,8},{10,9... | collective-permute-start | bytes 393224 | tf_op jit(solution)/shard_map/while/body/eval_jaxpr/ppermute | solution.py:52
  384.7 3.9 collective-permute-start
  395.3 7.2 %collective-permute-start.1 = (f32[1024,32]{0,1:T(8,128)S(1)}, f32[1024,32]{0,1:T(8,128)S(1)}, u32[]{:S(2)}, u32[]{:S(2)}) collective-permute-start(f32[1024,32]{0,1:T(8,128)S(1)} %get-tuple-element.496), channel_id=1, source_target_pairs={{0,15},{1,0},{2,1},{3,2},{4,3},{5,4},{6,5},{7,6},{8,7},{9,8},{10,9... | collective-permute-start | bytes 393224 | tf_op jit(solution)/shard_map/while/body/eval_jaxpr/ppermute | solution.py:52
  400.0 3.9 collective-permute-start
  410.6 7.2 %collective-permute-start.1 = (f32[1024,32]{0,1:T(8,128)S(1)}, f32[1024,32]{0,1:T(8,128)S(1)}, u32[]{:S(2)}, u32[]{:S(2)}) collective-permute-start(f32[1024,32]{0,1:T(8,128)S(1)} %get-tuple-element.496), channel_id=1, source_target_pairs={{0,15},{1,0},{2,1},{3,2},{4,3},{5,4},{6,5},{7,6},{8,7},{9,8},{10,9... | collective-permute-start | bytes 393224 | tf_op jit(solution)/shard_map/while/body/eval_jaxpr/ppermute | solution.py:52
  415.2 3.9 collective-permute-start
  425.9 7.2 %collective-permute-start.1 = (f32[1024,32]{0,1:T(8,128)S(1)}, f32[1024,32]{0,1:T(8,128)S(1)}, u32[]{:S(2)}, u32[]{:S(2)}) collective-permute-start(f32[1024,32]{0,1:T(8,128)S(1)} %get-tuple-element.496), channel_id=1, source_target_pairs={{0,15},{1,0},{2,1},{3,2},{4,3},{5,4},{6,5},{7,6},{8,7},{9,8},{10,9... | collective-permute-start | bytes 393224 | tf_op jit(solution)/shard_map/while/body/eval_jaxpr/ppermute | solution.py:52
  430.5 3.9 collective-permute-start
  441.1 7.2 %collective-permute-start.1 = (f32[1024,32]{0,1:T(8,128)S(1)}, f32[1024,32]{0,1:T(8,128)S(1)}, u32[]{:S(2)}, u32[]{:S(2)}) collective-permute-start(f32[1024,32]{0,1:T(8,128)S(1)} %get-tuple-element.496), channel_id=1, source_target_pairs={{0,15},{1,0},{2,1},{3,2},{4,3},{5,4},{6,5},{7,6},{8,7},{9,8},{10,9... | collective-permute-start | bytes 393224 | tf_op jit(solution)/shard_map/while/body/eval_jaxpr/ppermute | solution.py:52
  445.8 3.9 collective-permute-start
  456.4 7.2 %collective-permute-start.1 = (f32[1024,32]{0,1:T(8,128)S(1)}, f32[1024,32]{0,1:T(8,128)S(1)}, u32[]{:S(2)}, u32[]{:S(2)}) collective-permute-start(f32[1024,32]{0,1:T(8,128)S(1)} %get-tuple-element.496), channel_id=1, source_target_pairs={{0,15},{1,0},{2,1},{3,2},{4,3},{5,4},{6,5},{7,6},{8,7},{9,8},{10,9... | collective-permute-start | bytes 393224 | tf_op jit(solution)/shard_map/while/body/eval_jaxpr/ppermute | solution.py:52
  461.1 3.9 collective-permute-start
  471.7 7.2 %collective-permute-start.1 = (f32[1024,32]{0,1:T(8,128)S(1)}, f32[1024,32]{0,1:T(8,128)S(1)}, u32[]{:S(2)}, u32[]{:S(2)}) collective-permute-start(f32[1024,32]{0,1:T(8,128)S(1)} %get-tuple-element.496), channel_id=1, source_target_pairs={{0,15},{1,0},{2,1},{3,2},{4,3},{5,4},{6,5},{7,6},{8,7},{9,8},{10,9... | collective-permute-start | bytes 393224 | tf_op jit(solution)/shard_map/while/body/eval_jaxpr/ppermute | solution.py:52
  476.4 3.9 collective-permute-start
  487.0 7.2 %collective-permute-start.1 = (f32[1024,32]{0,1:T(8,128)S(1)}, f32[1024,32]{0,1:T(8,128)S(1)}, u32[]{:S(2)}, u32[]{:S(2)}) collective-permute-start(f32[1024,32]{0,1:T(8,128)S(1)} %get-tuple-element.496), channel_id=1, source_target_pairs={{0,15},{1,0},{2,1},{3,2},{4,3},{5,4},{6,5},{7,6},{8,7},{9,8},{10,9... | collective-permute-start | bytes 393224 | tf_op jit(solution)/shard_map/while/body/eval_jaxpr/ppermute | solution.py:52
  491.6 3.9 collective-permute-start
  (9 other events, 12.4 us)
where the time goes:
time: 498 us; the launch traced here: 496 us
  starting transfers between devices  153 us (31%)
  matrix products  139 us (28%)
  waiting for transfers between devices  121 us (24%)
  local copies, waits for them, and re-layouts  67.1 us (13%)
  loops' own time  11.6 us (2%)
    ppermute x32, starting transfers between devices, hop_body(): item_b = lax.ppermute(item_b, 'shard', send_perm)  150 us
    ppermute x32, waiting for transfers between devices, hop_body(): item_b = lax.ppermute(item_b, 'shard', send_perm)  78 us
    dot_general x256, matrix products, local_step(): lax.dot_general(user_low, item_low, (((1,), (1,)), ((), ())), preferred_e...  54 us
    dot_general x256, matrix products, local_step(): lax.dot_general(err_low, user_low, (((0,), (0,)), ((), ())), preferred_el...  46 us
    ppermute x32, waiting for transfers between devices, hop_body(): item_a = lax.ppermute(item_a, 'shard', send_perm)  42.7 us
    dot_general x256, matrix products, local_step(): jnp.dot(err_low, item_low, preferred_element_type=jnp.float32)  38.9 us
    dynamic_slice x32, local copies, waits for them, and re-layouts, hop_body(): lax.dynamic_slice_in_dim(ratings_b, col_start, item_blk, axis=1)  34.4 us
    dynamic_slice x32, local copies, waits for them, and re-layouts, hop_body(): flag_now_b = lax.dynamic_slice_in_dim(flags_b, col_start, item_blk, axis=1)  29.8 us
  transfers between devices with their start and end apart: 64, of which 64 were waited for; matrix products, arithmetic and copies ran while one was open for 0% of the time, Pallas kernels for 0%

commit v1 on v0

v1 whole, which is shorter than its diff:
```python
import functools
import math
import jax
import jax.numpy as jnp
from jax import lax
from jax.experimental import pallas as pl
from jax.experimental.pallas import tpu as pltpu
from jax.sharding import PartitionSpec as P

SWEEP_STEPS = 4
EPOCHS = 2
WEIGHT_DECAY = 0.05
CHUNK = 256
MESH = pl.DeviceIdType.MESH


def sweep(u_ref, v_ref, rate_ref, flag_ref, step_u, step_v):
    user = u_ref[...]
    user_low = user.astype(jnp.bfloat16)
    user_low_t = user.T.astype(jnp.bfloat16)
    grad_u = None
    for c in range(v_ref.shape[0]):
        cols = pl.ds(c * CHUNK, CHUNK)
        item = v_ref[c]
        item_low = item.astype(jnp.bfloat16)
        approx = jnp.dot(user_low, item_low, preferred_element_type=jnp.float32)
        err_low = (approx - rate_ref[:, cols]).astype(jnp.bfloat16) * flag_ref[:, cols]
        part = lax.dot_general(err_low, item_low, (((1,), (1,)), ((), ())), preferred_element_type=jnp.float32)
        grad_u = part if grad_u is None else grad_u + part
        grad_v = jnp.dot(user_low_t, err_low, preferred_element_type=jnp.float32)
        v_ref[c] = item - step_v * (grad_v + WEIGHT_DECAY * item)
    u_ref[...] = user - step_u * (grad_u + WEIGHT_DECAY * user)


def kernel(shards, step_u, step_v, ra, ma, ua, va, rb, mb, ub, vb, ua_o, va_o, ub_o, vb_o,
           rates, masks, flags, items, users, load_sem, first_sem, send_sem, recv_sem, out_sem):
    me = lax.axis_index("shard")
    left = lax.rem(me + shards - 1, shards)
    right = lax.rem(me + 1, shards)
    block = rates.shape[-1]
    chunks = block // CHUNK
    stages = EPOCHS * shards
    rate_in, mask_in = (ra, rb), (ma, mb)

    def loads(m, t):
        j = lax.rem(me + t, shards)
        cols = pl.ds(pl.multiple_of(j * block, block), block)
        return (pltpu.make_async_copy(rate_in[m].at[:, cols], rates.at[m, j], load_sem.at[0, m, j]),
                pltpu.make_async_copy(mask_in[m].at[:, cols], masks.at[m, j], load_sem.at[1, m, j]))

    def first(m, c):
        return pltpu.make_async_copy((va, vb)[m].at[:, pl.ds(c * CHUNK, CHUNK)], items.at[m, 0, c], first_sem.at[m, c])

    def last(m, c):
        return pltpu.make_async_copy(items.at[m, stages, c], (va_o, vb_o)[m].at[:, pl.ds(c * CHUNK, CHUNK)], out_sem.at[m, c])

    def hop(m, t):
        return pltpu.make_async_remote_copy(
            src_ref=items.at[m, t], dst_ref=items.at[m, t + 1], send_sem=send_sem.at[m],
            recv_sem=recv_sem.at[m, t + 1], device_id={"shard": left}, device_id_type=MESH)

    for m in range(2):
        for c in range(chunks):
            first(m, c).start()
        for cp in loads(m, 0):
            cp.start()

    barrier = pltpu.get_barrier_semaphore()
    for other in (left, right):
        pl.semaphore_signal(barrier, inc=1, device_id={"shard": other}, device_id_type=MESH)

    @pl.loop(1, shards)
    def _(t):
        for m in range(2):
            for cp in loads(m, t):
                cp.start()

    users[0] = ua[...].T
    users[1] = ub[...].T
    for m in range(2):
        for c in range(chunks):
            first(m, c).wait()
    pl.semaphore_wait(barrier, 2)

    @pl.loop(0, stages)
    def _(t):
        j = lax.rem(me + t, shards)
        for m in range(2):
            @pl.when(t < shards)
            def _():
                for cp in loads(m, t):
                    cp.wait()
            flags[m] = masks[m, j].astype(jnp.float32).astype(jnp.bfloat16)

            @pl.when(t > 0)
            def _():
                hop(m, t - 1).wait()

            @pl.loop(0, SWEEP_STEPS)
            def _(s):
                sweep(users.at[m], items.at[m, t], rates.at[m, j], flags.at[m], step_u, step_v)
            hop(m, t).start()

    ua_o[...] = users[0].T
    ub_o[...] = users[1].T
    for m in range(2):
        hop(m, stages - 1).wait()
        for c in range(chunks):
            last(m, c).start()
    for m in range(2):
        for c in range(chunks):
            last(m, c).wait()


def solution(mesh):
    shards = mesh.shape["shard"]
    row_spec = P(("rep", "shard"), None)

    def device_body(ratings_a, mask_a, users_a, items_a, ratings_b, mask_b, users_b, items_b):
        users_dev, rank = users_a.shape
        block = items_a.shape[0]
        chunks = block // CHUNK
        stages = EPOCHS * shards
        step_u = 0.5 * math.sqrt(rank) / (block + 2 * rank)
        step_v = 0.5 * math.sqrt(rank) / (users_dev + 2 * rank)
        hbm = pl.BlockSpec(memory_space=pl.ANY)
        vmem = pl.BlockSpec(memory_space=pltpu.VMEM)
        f32 = jnp.float32
        ut = jax.ShapeDtypeStruct((rank, users_dev), f32)
        vt = jax.ShapeDtypeStruct((rank, block), f32)
        outs = pl.pallas_call(
            functools.partial(kernel, shards, step_u, step_v),
            out_shape=(ut, vt, ut, vt),
            in_specs=[hbm, hbm, vmem, hbm] * 2,
            out_specs=[vmem, hbm] * 2,
            scratch_shapes=[
                pltpu.VMEM((2, shards, users_dev, block), f32),
                pltpu.VMEM((2, shards, users_dev, block), jnp.int32),
                pltpu.VMEM((2, users_dev, block), jnp.bfloat16),
                pltpu.VMEM((2, stages + 1, chunks, rank, CHUNK), f32),
                pltpu.VMEM((2, users_dev, rank), f32),
                pltpu.SemaphoreType.DMA((2, 2, shards)),
                pltpu.SemaphoreType.DMA((2, chunks)),
                pltpu.SemaphoreType.DMA((2,)),
                pltpu.SemaphoreType.DMA((2, stages + 1)),
                pltpu.SemaphoreType.DMA((2, chunks)),
            ],
            compiler_params=pltpu.CompilerParams(
                collective_id=0, has_side_effects=True, vmem_limit_bytes=48 * 1024 * 1024),
            name="sweep_ring",
        )(ratings_a, mask_a, users_a.T, items_a.T, ratings_b, mask_b, users_b.T, items_b.T)
        return tuple(o.T for o in outs)

    return jax.shard_map(device_body, mesh=mesh, in_specs=(row_spec,) * 8, out_specs=(row_spec,) * 4, check_vma=False)
```

time: 498 us -> 197 us (0.40)
  Pallas kernels: 0 us -> 188 us
  starting transfers between devices: 153 us -> 0 us
  matrix products: 139 us -> 0 us
  waiting for transfers between devices: 121 us -> 0 us
  local copies, waits for them, and re-layouts: 67.1 us -> 7.94 us
  loops' own time: 11.6 us -> 0 us
    pallas_call x0 -> x1, Pallas kernels: none -> 188 us  [device_body(): pl.pallas_call(functools.partial(kernel, shards, step_u, step_v), out_sha...]
    ppermute x64 -> x0, starting transfers between devices: 153 us -> none  [the longest x32 150 us: hop_body(): item_b = lax.ppermute(item_b, 'shard', send_perm)]
    dot_general x768 -> x0, matrix products: 139 us -> none  [the longest x256 54 us: local_step(): lax.dot_general(user_low, item_low, (((1,), (1,)), ((), ())), preferred_e...]
    ppermute x64 -> x0, waiting for transfers between devices: 121 us -> none  [the longest x32 78 us: hop_body(): item_b = lax.ppermute(item_b, 'shard', send_perm)]
    dynamic_slice x64 -> x0, local copies, waits for them, and re-layouts: 64.1 us -> none  [the longest x32 34.4 us: hop_body(): lax.dynamic_slice_in_dim(ratings_b, col_start, item_blk, axis=1)]
    another operation x33 -> x0, loops' own time: 11.6 us -> none  [the longest x32 9.53 us: hop_body(): lax.fori_loop(0, SWEEP_STEPS, one_step, (user_a, item_a, user_b, item_b))]
    unnamed x18 -> x14, local copies, waits for them, and re-layouts: 1.58 us -> 7.94 us
  transfers between devices with their start and end apart: 64 -> 0, of which waited for: 64 -> 0; matrix products, arithmetic and copies ran while one was open for 0% -> 0% of each run, Pallas kernels for 0% -> 0%
where the time goes in v1:
time: 197 us; the launch traced here: 196 us
  Pallas kernels  188 us (95%)
  local copies, waits for them, and re-layouts  7.94 us (4%)
    pallas_call x1, Pallas kernels, device_body(): pl.pallas_call(functools.partial(kernel, shards, step_u, step_v), out_sha...  188 us
    unnamed x14, local copies, waits for them, and re-layouts  7.94 us

profile of v1, /device:TPU:0, one launch (start us, length us, event | category | flops | bytes accessed | tf_op | source)
XLA Modules:
  0.0 196.2 jit_solution(14706675620585733151)
XLA Ops:
  0.6 0.0 copy-start
  0.6 2.2 %copy-done = f32[64,16384]{1,0:T(8,128)S(1)} copy-done((f32[64,16384]{1,0:T(8,128)S(1)}, f32[64,16384]{1,0:T(8,128)}, u32[]{:S(2)}) %copy-start) | copy-done | bytes 4194328
  2.8 0.0 copy-start.1
  2.8 0.9 copy-done.1
  3.7 0.0 copy-start.2
  3.7 0.9 copy-done.2
  4.6 0.0 copy-start.3
  4.6 0.7 copy-done.3
  5.3 0.0 copy-start.4
  5.4 0.7 copy-done.4
  6.1 187.6 %sweep_ring.1 = (f32[32,64]{1,0:T(8,128)S(1)}, f32[32,1024]{1,0:T(8,128)S(1)}, f32[32,64]{1,0:T(8,128)S(1)}, f32[32,1024]{1,0:T(8,128)S(1)}) custom-call(f32[64,16384]{1,0:T(8,128)S(1)} %copy-done, s32[64,16384]{1,0:T(8,128)} %ma.1, f32[32,64]{1,0:T(8,128)S(1)} %bitcast.14, f32[32,1024]{1,0:T(8,128)S(1)} %bitcast.8, f32[64,16384]{1,0:T(8,128)} %rb.1, ...), custom_call_target="tpu_custom_call" | custom-call | tf_op jit(solution)/shard_map/sweep_ring/pallas_call | solution.py:131
  193.7 0.6 copy.16
  194.3 0.7 copy.17
  195.0 0.6 copy.18
  195.6 0.7 copy.19
Async XLA Ops:
  0.6 2.2 %copy-start = (f32[64,16384]{1,0:T(8,128)S(1)}, f32[64,16384]{1,0:T(8,128)}, u32[]{:S(2)}) copy-start(f32[64,16384]{1,0:T(8,128)} %ra.1) | copy-start | bytes 12582916
  2.8 0.9 copy-start.1
  3.7 0.9 copy-start.2
  4.6 0.7 copy-start.3
  5.3 0.7 copy-start.4

commit v2 on v1

--- a/solution.py
+++ b/solution.py
@@ -56,7 +56,7 @@
 
     def hop(m, t):
         return pltpu.make_async_remote_copy(
-            src_ref=items.at[m, t], dst_ref=items.at[m, t + 1], send_sem=send_sem.at[m],
+            src_ref=items.at[m, t], dst_ref=items.at[m, t + 1], send_sem=send_sem.at[m, t],
             recv_sem=recv_sem.at[m, t + 1], device_id={"shard": left}, device_id_type=MESH)
 
     for m in range(2):
@@ -94,7 +94,7 @@
 
             @pl.when(t > 0)
             def _():
-                hop(m, t - 1).wait()
+                hop(m, t - 1).wait_recv()
 
             @pl.loop(0, SWEEP_STEPS)
             def _(s):
@@ -104,12 +104,17 @@
     ua_o[...] = users[0].T
     ub_o[...] = users[1].T
     for m in range(2):
-        hop(m, stages - 1).wait()
+        hop(m, stages - 1).wait_recv()
         for c in range(chunks):
             last(m, c).start()
     for m in range(2):
         for c in range(chunks):
             last(m, c).wait()
+
+    @pl.loop(0, stages)
+    def _(t):
+        for m in range(2):
+            hop(m, t).wait_send()
 
 
 def solution(mesh):
@@ -123,7 +128,7 @@
         stages = EPOCHS * shards
         step_u = 0.5 * math.sqrt(rank) / (block + 2 * rank)
         step_v = 0.5 * math.sqrt(rank) / (users_dev + 2 * rank)
-        hbm = pl.BlockSpec(memory_space=pl.ANY)
+        hbm = pl.BlockSpec(memory_space=pltpu.HBM)
         vmem = pl.BlockSpec(memory_space=pltpu.VMEM)
         f32 = jnp.float32
         ut = jax.ShapeDtypeStruct((rank, users_dev), f32)
@@ -141,7 +146,7 @@
                 pltpu.VMEM((2, users_dev, rank), f32),
                 pltpu.SemaphoreType.DMA((2, 2, shards)),
                 pltpu.SemaphoreType.DMA((2, chunks)),
-                pltpu.SemaphoreType.DMA((2,)),
+                pltpu.SemaphoreType.DMA((2, stages)),
                 pltpu.SemaphoreType.DMA((2, stages + 1)),
                 pltpu.SemaphoreType.DMA((2, chunks)),
             ],

time: 197 us -> 197 us (level)
  no operation moved by 1% of the time
where the time goes in v2:
time: 197 us
  Pallas kernels  188 us (95%)
  local copies, waits for them, and re-layouts  7.94 us (4%)
    pallas_call x1, Pallas kernels, device_body(): pl.pallas_call(functools.partial(kernel, shards, step_u, step_v), out_sha...  188 us
    unnamed x14, local copies, waits for them, and re-layouts  7.94 us

profile of v2, /device:TPU:0, one launch (start us, length us, event | category | flops | bytes accessed | tf_op | source)
XLA Modules:
  0.0 196.7 jit_solution(10196159117212900528)
XLA Ops:
  0.6 0.0 copy-start
  0.6 2.2 %copy-done = f32[64,16384]{1,0:T(8,128)S(1)} copy-done((f32[64,16384]{1,0:T(8,128)S(1)}, f32[64,16384]{1,0:T(8,128)}, u32[]{:S(2)}) %copy-start) | copy-done | bytes 4194328
  2.8 0.0 copy-start.1
  2.8 0.9 copy-done.1
  3.7 0.0 copy-start.2
  3.7 0.9 copy-done.2
  4.6 0.0 copy-start.3
  4.6 0.7 copy-done.3
  5.3 0.0 copy-start.4
  5.4 0.7 copy-done.4
  6.1 188.1 %sweep_ring.1 = (f32[32,64]{1,0:T(8,128)S(1)}, f32[32,1024]{1,0:T(8,128)S(1)}, f32[32,64]{1,0:T(8,128)S(1)}, f32[32,1024]{1,0:T(8,128)S(1)}) custom-call(f32[64,16384]{1,0:T(8,128)S(1)} %copy-done, s32[64,16384]{1,0:T(8,128)} %ma.1, f32[32,64]{1,0:T(8,128)S(1)} %bitcast.14, f32[32,1024]{1,0:T(8,128)S(1)} %bitcast.8, f32[64,16384]{1,0:T(8,128)} %rb.1, ...), custom_call_target="tpu_custom_call" | custom-call | tf_op jit(solution)/shard_map/sweep_ring/pallas_call | solution.py:136
  194.2 0.6 copy.16
  194.8 0.7 copy.17
  195.5 0.6 copy.18
  196.1 0.7 copy.19
Async XLA Ops:
  0.6 2.2 %copy-start = (f32[64,16384]{1,0:T(8,128)S(1)}, f32[64,16384]{1,0:T(8,128)}, u32[]{:S(2)}) copy-start(f32[64,16384]{1,0:T(8,128)} %ra.1) | copy-start | bytes 12582916
  2.8 0.9 copy-start.1
  3.7 0.9 copy-start.2
  4.6 0.7 copy-start.3
  5.3 0.7 copy-start.4

commit v3 on v1

v3 whole, which is shorter than its diff:
```python
import functools
import math
import jax
import jax.numpy as jnp
from jax import lax
from jax.experimental import pallas as pl
from jax.experimental.pallas import tpu as pltpu
from jax.sharding import PartitionSpec as P

SWEEP_STEPS = 4
EPOCHS = 2
WEIGHT_DECAY = 0.05
CHUNK = 256
MESH = pl.DeviceIdType.MESH


def sweep(u_ref, v_ref, rate_ref, flag_ref, step_u, step_v):
    user = u_ref[...]
    user_low = user.astype(jnp.bfloat16)
    user_low_t = user.T.astype(jnp.bfloat16)
    grad_u = None
    for c in range(v_ref.shape[0]):
        cols = pl.ds(c * CHUNK, CHUNK)
        item = v_ref[c]
        item_low = item.astype(jnp.bfloat16)
        approx = jnp.dot(user_low, item_low, preferred_element_type=jnp.float32)
        err_low = (approx - rate_ref[:, cols]).astype(jnp.bfloat16) * flag_ref[:, cols]
        part = lax.dot_general(err_low, item_low, (((1,), (1,)), ((), ())), preferred_element_type=jnp.float32)
        grad_u = part if grad_u is None else grad_u + part
        grad_v = jnp.dot(user_low_t, err_low, preferred_element_type=jnp.float32)
        v_ref[c] = item - step_v * (grad_v + WEIGHT_DECAY * item)
    u_ref[...] = user - step_u * (grad_u + WEIGHT_DECAY * user)


def kernel(shards, step_u, step_v, ra, ma, ua, va, rb, mb, ub, vb, ua_o, va_o, ub_o, vb_o,
           rates, masks, flags, items, last_items, users, users_in, users_out,
           load_sem, push_sem, send_sem, recv_sem, last_sem, user_sem, out_sem):
    me = lax.axis_index("shard")
    core = lax.rem(me, 2)
    base = me - core
    peer = base + 1 - core
    block = rates.shape[-1]
    chunks = block // CHUNK
    stages = EPOCHS * shards

    def dev(index):
        return {"shard": lax.rem(index + shards, shards)}

    def own(k):
        return (ra, ma, ua, va) if k == 0 else (rb, mb, ub, vb)

    def span(j):
        return pl.ds(pl.multiple_of(j * block, block), block)

    def pieces(k, q):
        j = lax.rem(base + k + q, shards)
        out = []
        for kind, buf in ((0, rates), (1, masks)):
            out.append(pltpu.make_async_copy(own(k)[kind].at[:, span(j)], buf.at[k, j], load_sem.at[kind, k, j]))
            out.append(pltpu.make_async_remote_copy(
                src_ref=own(1 - k)[kind].at[:, span(j)], dst_ref=buf.at[k, j], send_sem=push_sem.at[kind, j],
                recv_sem=load_sem.at[kind, k, j], device_id=dev(peer), device_id_type=MESH))
        return out

    def firsts(k):
        out = []
        for c in range(chunks):
            cols = pl.ds(c * CHUNK, CHUNK)
            out.append((pltpu.make_async_copy(own(k)[3].at[:, cols], items.at[k, c], recv_sem.at[k]),
                        pltpu.make_async_remote_copy(
                            src_ref=own(1 - k)[3].at[:, cols], dst_ref=items.at[k, c], send_sem=last_sem.at[2],
                            recv_sem=recv_sem.at[k], device_id=dev(peer), device_id_type=MESH)))
        return out

    def user_push(k):
        return pltpu.make_async_remote_copy(
            src_ref=own(1 - k)[2], dst_ref=users_in, send_sem=user_sem.at[0], recv_sem=user_sem.at[1],
            device_id=dev(peer), device_id_type=MESH)

    def hop(s):
        return pltpu.make_async_remote_copy(
            src_ref=items.at[s], dst_ref=items.at[s + 2], send_sem=send_sem.at[s],
            recv_sem=recv_sem.at[s + 2], device_id=dev(me - 2), device_id_type=MESH)

    def home(s, target):
        return pltpu.make_async_remote_copy(
            src_ref=items.at[s], dst_ref=last_items.at[core], send_sem=send_sem.at[s],
            recv_sem=last_sem.at[core], device_id=dev(target), device_id_type=MESH)

    def user_home(k):
        return pltpu.make_async_remote_copy(
            src_ref=users.at[1 - k], dst_ref=users_out, send_sem=user_sem.at[2], recv_sem=user_sem.at[3],
            device_id=dev(peer), device_id_type=MESH)

    def landed(s):
        return pltpu.make_async_copy(items.at[s], items.at[s], recv_sem.at[s])

    barrier = pltpu.get_barrier_semaphore()
    for step in (-2, -1, 1, 2):
        pl.semaphore_signal(barrier, inc=1, device_id=dev(me + step), device_id_type=MESH)
    pl.semaphore_wait(barrier, 4)

    for k in range(2):
        @pl.when(core == k)
        def _():
            user_push(k).start()
            for here, there in firsts(k):
                here.start()
                there.start()
            users[k] = own(k)[2][...].T

            @pl.loop(0, shards)
            def _(q):
                for cp in pieces(k, q):
                    cp.start()

    for k in range(2):
        @pl.when(core == k)
        def _():
            user_push(k).wait_recv()
            users[1 - k] = users_in[...].T

    def ready(role, j):
        for kind, buf in ((0, rates), (1, masks)):
            pltpu.make_async_copy(buf.at[role, j], buf.at[role, j], load_sem.at[kind, role, j]).wait()

    def visit(role, s, j):
        @pl.loop(0, SWEEP_STEPS)
        def _(n):
            sweep(users.at[role], items.at[s], rates.at[role, j], flags.at[role], step_u, step_v)

    @pl.loop(0, stages + 1)
    def _(s):
        j = lax.rem(base + s, shards)

        @pl.when(s < shards)
        def _():
            ready(0, j)

        @pl.when(jnp.logical_and(s >= 1, s <= shards))
        def _():
            ready(1, j)

        flags[0] = masks[0, j].astype(jnp.float32).astype(jnp.bfloat16)

        @pl.when(s > 0)
        def _():
            flags[1] = masks[1, j].astype(jnp.float32).astype(jnp.bfloat16)

        landed(s).wait()

        @pl.when(s > 0)
        def _():
            visit(1, s, j)

        @pl.when(s < stages)
        def _():
            visit(0, s, j)

        @pl.when(s < stages - 1)
        def _():
            hop(s).start()

        @pl.when(s == stages - 1)
        def _():
            home(s, base - 1).start()

    for k in range(2):
        @pl.when(core == k)
        def _():
            user_home(k).start()
            (ua_o, ub_o)[k][...] = users[k].T

    @pl.when(core == 1)
    def _():
        home(stages, base).start()

    def outs(k):
        got = []
        for m in range(2):
            src = items.at[stages] if (k == 0 and m == 0) else last_items.at[m]
            for c in range(chunks):
                got.append(pltpu.make_async_copy(src.at[c], (va_o, vb_o)[m].at[:, pl.ds(c * CHUNK, CHUNK)], out_sem.at[m, c]))
        return got

    for k in range(2):
        @pl.when(core == k)
        def _():
            for m in range(2):
                if k or m:
                    pltpu.make_async_copy(last_items.at[m], last_items.at[m], last_sem.at[m]).wait()
            for cp in outs(k):
                cp.start()
            user_home(k).wait()
            (ua_o, ub_o)[1 - k][...] = users_out[...].T
            for cp in outs(k):
                cp.wait()
            user_push(k).wait_send()
            pltpu.make_async_copy(items.at[k], items.at[k], last_sem.at[2]).wait()

            @pl.loop(0, shards)
            def _(q):
                for cp in pieces(k, q)[1::2]:
                    cp.wait_send()

    @pl.loop(0, stages)
    def _(s):
        pltpu.make_async_copy(items.at[s], items.at[s], send_sem.at[s]).wait()

    @pl.when(core == 1)
    def _():
        home(stages, base).wait_send()


def solution(mesh):
    shards = mesh.shape["shard"]
    row_spec = P(("rep", "shard"), None)

    def device_body(ratings_a, mask_a, users_a, items_a, ratings_b, mask_b, users_b, items_b):
        users_dev, rank = users_a.shape
        block = items_a.shape[0]
        chunks = block // CHUNK
        stages = EPOCHS * shards
        step_u = 0.5 * math.sqrt(rank) / (block + 2 * rank)
        step_v = 0.5 * math.sqrt(rank) / (users_dev + 2 * rank)
        hbm = pl.BlockSpec(memory_space=pltpu.HBM)
        vmem = pl.BlockSpec(memory_space=pltpu.VMEM)
        f32 = jnp.float32
        ut = jax.ShapeDtypeStruct((rank, users_dev), f32)
        vt = jax.ShapeDtypeStruct((rank, block), f32)
        outs = pl.pallas_call(
            functools.partial(kernel, shards, step_u, step_v),
            out_shape=(ut, vt, ut, vt),
            in_specs=[hbm, hbm, vmem, hbm] * 2,
            out_specs=[vmem, hbm] * 2,
            scratch_shapes=[
                pltpu.VMEM((2, shards, users_dev, block), f32),
                pltpu.VMEM((2, shards, users_dev, block), jnp.int32),
                pltpu.VMEM((2, users_dev, block), jnp.bfloat16),
                pltpu.VMEM((stages + 1, chunks, rank, CHUNK), f32),
                pltpu.VMEM((2, chunks, rank, CHUNK), f32),
                pltpu.VMEM((2, users_dev, rank), f32),
                pltpu.VMEM((rank, users_dev), f32),
                pltpu.VMEM((users_dev, rank), f32),
                pltpu.SemaphoreType.DMA((2, 2, shards)),
                pltpu.SemaphoreType.DMA((2, shards)),
                pltpu.SemaphoreType.DMA((stages + 1,)),
                pltpu.SemaphoreType.DMA((stages + 1,)),
                pltpu.SemaphoreType.DMA((3,)),
                pltpu.SemaphoreType.DMA((4,)),
                pltpu.SemaphoreType.DMA((2, chunks)),
            ],
            compiler_params=pltpu.CompilerParams(
                collective_id=0, has_side_effects=True, vmem_limit_bytes=62 * 1024 * 1024),
            name="sweep_ring",
        )(ratings_a, mask_a, users_a.T, items_a.T, ratings_b, mask_b, users_b.T, items_b.T)
        return tuple(o.T for o in outs)

    return jax.shard_map(device_body, mesh=mesh, in_specs=(row_spec,) * 8, out_specs=(row_spec,) * 4, check_vma=False)
```

time: 197 us -> 199 us (1.010)
  Pallas kernels: 188 us -> 192 us
  local copies, waits for them, and re-layouts: 7.94 us -> 5.78 us
    pallas_call x1, Pallas kernels: 188 us -> 192 us  [device_body(): pl.pallas_call(functools.partial(kernel, shards, step_u, step_v), out_sha...]
    unnamed x14 -> x4, local copies, waits for them, and re-layouts: 7.94 us -> 5.78 us
where the time goes in v3:
time: 199 us; the launch traced here: 198 us
  Pallas kernels  192 us (96%)
  local copies, waits for them, and re-layouts  5.78 us (3%)
    pallas_call x1, Pallas kernels, device_body(): pl.pallas_call(functools.partial(kernel, shards, step_u, step_v), out_sha...  192 us
    unnamed x4, local copies, waits for them, and re-layouts  5.78 us

profile of v3, /device:TPU:0, one launch (start us, length us, event | category | flops | bytes accessed | tf_op | source)
XLA Modules:
  0.0 198.3 jit_solution(7620917774514984354)
XLA Ops:
  0.6 191.9 %sweep_ring.1 = (f32[32,64]{1,0:T(8,128)}, f32[32,1024]{1,0:T(8,128)}, f32[32,64]{1,0:T(8,128)}, f32[32,1024]{1,0:T(8,128)}) custom-call(f32[64,16384]{1,0:T(8,128)} %ra.1, s32[64,16384]{1,0:T(8,128)} %ma.1, f32[32,64]{1,0:T(8,128)} %bitcast.14, f32[32,1024]{1,0:T(8,128)} %bitcast.8, f32[64,16384]{1,0:T(8,128)} %rb.1, s32[64,16384]{1,0:T(8,128)} %mb.1, ...), custom_call_target="tpu_custom_call" | custom-call | tf_op jit(solution)/shard_map/sweep_ring/pallas_call | solution.py:231
  192.5 1.3 copy.16
  193.9 1.6 copy.17
  195.4 1.3 copy.18
  196.7 1.6 copy.19

commit v4 on v3

--- a/solution.py
+++ b/solution.py
@@ -15,20 +15,23 @@
 
 
 def sweep(u_ref, v_ref, rate_ref, flag_ref, step_u, step_v):
+    chunks = range(v_ref.shape[0])
+    f32, bf16 = jnp.float32, jnp.bfloat16
     user = u_ref[...]
-    user_low = user.astype(jnp.bfloat16)
-    user_low_t = user.T.astype(jnp.bfloat16)
-    grad_u = None
-    for c in range(v_ref.shape[0]):
+    user_low = user.astype(bf16)
+    user_low_t = user.T.astype(bf16)
+    item_low = [v_ref[c].astype(bf16) for c in chunks]
+    approx = [jnp.dot(user_low, item_low[c], preferred_element_type=f32) for c in chunks]
+    err_low = []
+    for c in chunks:
         cols = pl.ds(c * CHUNK, CHUNK)
+        err_low.append((approx[c] - rate_ref[:, cols]).astype(bf16) * flag_ref[:, cols])
+    part = [lax.dot_general(err_low[c], item_low[c], (((1,), (1,)), ((), ())), preferred_element_type=f32) for c in chunks]
+    grad_v = [jnp.dot(user_low_t, err_low[c], preferred_element_type=f32) for c in chunks]
+    for c in chunks:
         item = v_ref[c]
-        item_low = item.astype(jnp.bfloat16)
-        approx = jnp.dot(user_low, item_low, preferred_element_type=jnp.float32)
-        err_low = (approx - rate_ref[:, cols]).astype(jnp.bfloat16) * flag_ref[:, cols]
-        part = lax.dot_general(err_low, item_low, (((1,), (1,)), ((), ())), preferred_element_type=jnp.float32)
-        grad_u = part if grad_u is None else grad_u + part
-        grad_v = jnp.dot(user_low_t, err_low, preferred_element_type=jnp.float32)
-        v_ref[c] = item - step_v * (grad_v + WEIGHT_DECAY * item)
+        v_ref[c] = item - step_v * (grad_v[c] + WEIGHT_DECAY * item)
+    grad_u = (part[0] + part[1]) + (part[2] + part[3])
     u_ref[...] = user - step_u * (grad_u + WEIGHT_DECAY * user)
 
 

time: 199 us -> 142 us (0.71)
  Pallas kernels: 192 us -> 134 us
    pallas_call x1, Pallas kernels: 192 us -> 134 us  [device_body(): pl.pallas_call(functools.partial(kernel, shards, step_u, step_v), out_sha...]
where the time goes in v4:
time: 142 us; the launch traced here: 141 us
  Pallas kernels  134 us (94%)
  local copies, waits for them, and re-layouts  5.78 us (4%)
    pallas_call x1, Pallas kernels, device_body(): pl.pallas_call(functools.partial(kernel, shards, step_u, step_v), out_sha...  134 us
    unnamed x4, local copies, waits for them, and re-layouts  5.78 us

profile of v4, /device:TPU:0, one launch (start us, length us, event | category | flops | bytes accessed | tf_op | source)
XLA Modules:
  0.0 140.7 jit_solution(525269550163342860)
XLA Ops:
  0.6 134.3 %sweep_ring.1 = (f32[32,64]{1,0:T(8,128)}, f32[32,1024]{1,0:T(8,128)}, f32[32,64]{1,0:T(8,128)}, f32[32,1024]{1,0:T(8,128)}) custom-call(f32[64,16384]{1,0:T(8,128)} %ra.1, s32[64,16384]{1,0:T(8,128)} %ma.1, f32[32,64]{1,0:T(8,128)} %bitcast.14, f32[32,1024]{1,0:T(8,128)} %bitcast.8, f32[64,16384]{1,0:T(8,128)} %rb.1, s32[64,16384]{1,0:T(8,128)} %mb.1, ...), custom_call_target="tpu_custom_call" | custom-call | tf_op jit(solution)/shard_map/sweep_ring/pallas_call | solution.py:234
  134.9 1.3 copy.16
  136.3 1.6 %copy.17 = f32[1024,32]{0,1:T(8,128)} copy(f32[1024,32]{0,1:T(8,128)} %bitcast.11) | data formatting | bytes 262144
  137.8 1.3 copy.18
  139.1 1.6 %copy.19 = f32[1024,32]{0,1:T(8,128)} copy(f32[1024,32]{0,1:T(8,128)} %bitcast.10) | data formatting | bytes 262144

commit v5 on v4

--- a/solution.py
+++ b/solution.py
@@ -11,6 +11,8 @@
 EPOCHS = 2
 WEIGHT_DECAY = 0.05
 CHUNK = 256
+AHEAD = 3
+STAGGER = 1500
 MESH = pl.DeviceIdType.MESH
 
 
@@ -101,6 +103,17 @@
     barrier = pltpu.get_barrier_semaphore()
     for step in (-2, -1, 1, 2):
         pl.semaphore_signal(barrier, inc=1, device_id=dev(me + step), device_id_type=MESH)
+
+    for k in range(2):
+        @pl.when(core == k)
+        def _():
+            for here, there in firsts(k):
+                here.start()
+            for q in range(AHEAD):
+                for cp in pieces(k, q)[0::2]:
+                    cp.start()
+            users[k] = own(k)[2][...].T
+
     pl.semaphore_wait(barrier, 4)
 
     for k in range(2):
@@ -108,13 +121,9 @@
         def _():
             user_push(k).start()
             for here, there in firsts(k):
-                here.start()
                 there.start()
-            users[k] = own(k)[2][...].T
-
-            @pl.loop(0, shards)
-            def _(q):
-                for cp in pieces(k, q):
+            for q in range(AHEAD):
+                for cp in pieces(k, q)[1::2]:
                     cp.start()
 
     for k in range(2):
@@ -132,9 +141,19 @@
         def _(n):
             sweep(users.at[role], items.at[s], rates.at[role, j], flags.at[role], step_u, step_v)
 
+    @pl.when(core == 1)
+    def _():
+        pl.delay(STAGGER)
+
     @pl.loop(0, stages + 1)
     def _(s):
         j = lax.rem(base + s, shards)
+
+        for k in range(2):
+            @pl.when(jnp.logical_and(core == k, s + AHEAD < shards))
+            def _():
+                for cp in pieces(k, s + AHEAD):
+                    cp.start()
 
         @pl.when(s < shards)
         def _():
@@ -213,6 +232,15 @@
     @pl.when(core == 1)
     def _():
         home(stages, base).wait_send()
+
+
+def place(ua, va, ub, vb, ua_o, va_o, ub_o, vb_o, sem):
+    copies = [pltpu.make_async_copy(src, dst, sem.at[i])
+              for i, (src, dst) in enumerate(((ua, ua_o), (va, va_o), (ub, ub_o), (vb, vb_o)))]
+    for cp in copies:
+        cp.start()
+    for cp in copies:
+        cp.wait()
 
 
 def solution(mesh):
@@ -235,7 +263,7 @@
             functools.partial(kernel, shards, step_u, step_v),
             out_shape=(ut, vt, ut, vt),
             in_specs=[hbm, hbm, vmem, hbm] * 2,
-            out_specs=[vmem, hbm] * 2,
+            out_specs=[vmem] * 4,
             scratch_shapes=[
                 pltpu.VMEM((2, shards, users_dev, block), f32),
                 pltpu.VMEM((2, shards, users_dev, block), jnp.int32),
@@ -254,9 +282,18 @@
                 pltpu.SemaphoreType.DMA((2, chunks)),
             ],
             compiler_params=pltpu.CompilerParams(
-                collective_id=0, has_side_effects=True, vmem_limit_bytes=62 * 1024 * 1024),
+                collective_id=0, has_side_effects=True, vmem_limit_bytes=60 * 1024 * 1024),
             name="sweep_ring",
         )(ratings_a, mask_a, users_a.T, items_a.T, ratings_b, mask_b, users_b.T, items_b.T)
+        outs = pl.pallas_call(
+            place,
+            out_shape=(ut, vt, ut, vt),
+            in_specs=[vmem] * 4,
+            out_specs=[pl.BlockSpec(memory_space=pl.ANY)] * 4,
+            scratch_shapes=[pltpu.SemaphoreType.DMA((4,))],
+            compiler_params=pltpu.CompilerParams(vmem_limit_bytes=60 * 1024 * 1024),
+            name="place",
+        )(*outs)
         return tuple(o.T for o in outs)
 
     return jax.shard_map(device_body, mesh=mesh, in_specs=(row_spec,) * 8, out_specs=(row_spec,) * 4, check_vma=False)

time: 142 us -> 137 us (0.965)
  local copies, waits for them, and re-layouts: 5.78 us -> 0 us
  Pallas kernels: 134 us -> 136 us
    unnamed x4 -> x0, local copies, waits for them, and re-layouts: 5.78 us -> none
    pallas_call x0 -> x1, Pallas kernels: none -> 1.75 us  [device_body(): pl.pallas_call(place, out_shape=(ut, vt, ut, vt), in_specs=[vmem] * 4, ou...]
where the time goes in v5:
time: 137 us; the launch traced here: 136 us
  Pallas kernels  136 us (99%)
    pallas_call x1, Pallas kernels, device_body(): pl.pallas_call(functools.partial(kernel, shards, step_u, step_v), out_sha...  134 us

profile of v5, /device:TPU:0, one launch (start us, length us, event | category | flops | bytes accessed | tf_op | source)
XLA Modules:
  0.0 136.2 jit_solution(12100823898365055119)
XLA Ops:
  0.6 133.8 %sweep_ring.1 = (f32[32,64]{1,0:T(8,128)}, f32[32,1024]{1,0:T(8,128)}, f32[32,64]{1,0:T(8,128)}, f32[32,1024]{1,0:T(8,128)}) custom-call(f32[64,16384]{1,0:T(8,128)} %ra.1, s32[64,16384]{1,0:T(8,128)} %ma.1, f32[32,64]{1,0:T(8,128)} %bitcast.10, f32[32,1024]{1,0:T(8,128)} %bitcast.8, f32[64,16384]{1,0:T(8,128)} %rb.1, s32[64,16384]{1,0:T(8,128)} %mb.1, ...), custom_call_target="tpu_custom_call" | custom-call | tf_op jit(solution)/shard_map/sweep_ring/pallas_call | solution.py:262
  134.5 1.7 %place.1 = (f32[32,64]{1,0:T(8,128)}, f32[32,1024]{1,0:T(8,128)}, f32[32,64]{1,0:T(8,128)}, f32[32,1024]{1,0:T(8,128)}) custom-call(f32[32,64]{1,0:T(8,128)} %get-tuple-element.12.ua, f32[32,1024]{1,0:T(8,128)} %get-tuple-element.13.va, f32[32,64]{1,0:T(8,128)} %get-tuple-element.14.ub, f32[32,1024]{1,0:T(8,128)} %get-tuple-element.15.vb), custom_call_target="tpu_custom_call" | custom-call | tf_op jit(solution)/shard_map/place/pallas_call | solution.py:288

commit v6 on v5

--- a/solution.py
+++ b/solution.py
@@ -12,7 +12,6 @@
 WEIGHT_DECAY = 0.05
 CHUNK = 256
 AHEAD = 3
-STAGGER = 1500
 MESH = pl.DeviceIdType.MESH
 
 
@@ -43,6 +42,7 @@
     me = lax.axis_index("shard")
     core = lax.rem(me, 2)
     base = me - core
+    market = lax.rem(core + base // 2, 2)
     peer = base + 1 - core
     block = rates.shape[-1]
     chunks = block // CHUNK
@@ -51,86 +51,83 @@
     def dev(index):
         return {"shard": lax.rem(index + shards, shards)}
 
-    def own(k):
-        return (ra, ma, ua, va) if k == 0 else (rb, mb, ub, vb)
+    def own(m):
+        return (ra, ma, ua, va) if m == 0 else (rb, mb, ub, vb)
 
     def span(j):
         return pl.ds(pl.multiple_of(j * block, block), block)
 
-    def pieces(k, q):
-        j = lax.rem(base + k + q, shards)
+    def pieces(m, q):
+        j = lax.rem(base + core + q, shards)
         out = []
         for kind, buf in ((0, rates), (1, masks)):
-            out.append(pltpu.make_async_copy(own(k)[kind].at[:, span(j)], buf.at[k, j], load_sem.at[kind, k, j]))
+            out.append(pltpu.make_async_copy(own(m)[kind].at[:, span(j)], buf.at[core, j], load_sem.at[kind, core, j]))
             out.append(pltpu.make_async_remote_copy(
-                src_ref=own(1 - k)[kind].at[:, span(j)], dst_ref=buf.at[k, j], send_sem=push_sem.at[kind, j],
-                recv_sem=load_sem.at[kind, k, j], device_id=dev(peer), device_id_type=MESH))
+                src_ref=own(1 - m)[kind].at[:, span(j)], dst_ref=buf.at[core, j], send_sem=push_sem.at[kind, j],
+                recv_sem=load_sem.at[kind, core, j], device_id=dev(peer), device_id_type=MESH))
         return out
 
-    def firsts(k):
+    def firsts(m):
         out = []
         for c in range(chunks):
             cols = pl.ds(c * CHUNK, CHUNK)
-            out.append((pltpu.make_async_copy(own(k)[3].at[:, cols], items.at[k, c], recv_sem.at[k]),
+            out.append((pltpu.make_async_copy(own(m)[3].at[:, cols], items.at[core, c], recv_sem.at[core]),
                         pltpu.make_async_remote_copy(
-                            src_ref=own(1 - k)[3].at[:, cols], dst_ref=items.at[k, c], send_sem=last_sem.at[2],
-                            recv_sem=recv_sem.at[k], device_id=dev(peer), device_id_type=MESH)))
+                            src_ref=own(1 - m)[3].at[:, cols], dst_ref=items.at[core, c], send_sem=last_sem.at[2],
+                            recv_sem=recv_sem.at[core], device_id=dev(peer), device_id_type=MESH)))
         return out
 
-    def user_push(k):
-        return pltpu.make_async_remote_copy(
-            src_ref=own(1 - k)[2], dst_ref=users_in, send_sem=user_sem.at[0], recv_sem=user_sem.at[1],
+    def user_push(m):
+        return pltpu.make_async_remote_copy(
+            src_ref=own(1 - m)[2], dst_ref=users_in, send_sem=user_sem.at[0], recv_sem=user_sem.at[1],
             device_id=dev(peer), device_id_type=MESH)
 
     def hop(s):
         return pltpu.make_async_remote_copy(
             src_ref=items.at[s], dst_ref=items.at[s + 2], send_sem=send_sem.at[s],
-            recv_sem=recv_sem.at[s + 2], device_id=dev(me - 2), device_id_type=MESH)
+            recv_sem=recv_sem.at[s + 2], device_id=dev(base - 1 - core), device_id_type=MESH)
 
     def home(s, target):
         return pltpu.make_async_remote_copy(
-            src_ref=items.at[s], dst_ref=last_items.at[core], send_sem=send_sem.at[s],
-            recv_sem=last_sem.at[core], device_id=dev(target), device_id_type=MESH)
-
-    def user_home(k):
-        return pltpu.make_async_remote_copy(
-            src_ref=users.at[1 - k], dst_ref=users_out, send_sem=user_sem.at[2], recv_sem=user_sem.at[3],
+            src_ref=items.at[s], dst_ref=last_items.at[market], send_sem=send_sem.at[s],
+            recv_sem=last_sem.at[market], device_id=dev(target), device_id_type=MESH)
+
+    def user_home():
+        return pltpu.make_async_remote_copy(
+            src_ref=users.at[1 - core], dst_ref=users_out, send_sem=user_sem.at[2], recv_sem=user_sem.at[3],
             device_id=dev(peer), device_id_type=MESH)
 
     def landed(s):
         return pltpu.make_async_copy(items.at[s], items.at[s], recv_sem.at[s])
 
     barrier = pltpu.get_barrier_semaphore()
-    for step in (-2, -1, 1, 2):
-        pl.semaphore_signal(barrier, inc=1, device_id=dev(me + step), device_id_type=MESH)
-
-    for k in range(2):
-        @pl.when(core == k)
-        def _():
-            for here, there in firsts(k):
+    for other in (base - 2, base - 1, peer, base + 2, base + 3):
+        pl.semaphore_signal(barrier, inc=1, device_id=dev(other), device_id_type=MESH)
+
+    for m in range(2):
+        @pl.when(market == m)
+        def _():
+            for here, there in firsts(m):
                 here.start()
             for q in range(AHEAD):
-                for cp in pieces(k, q)[0::2]:
+                for cp in pieces(m, q)[0::2]:
                     cp.start()
-            users[k] = own(k)[2][...].T
-
-    pl.semaphore_wait(barrier, 4)
-
-    for k in range(2):
-        @pl.when(core == k)
-        def _():
-            user_push(k).start()
-            for here, there in firsts(k):
+            users[core] = own(m)[2][...].T
+
+    pl.semaphore_wait(barrier, 5)
+
+    for m in range(2):
+        @pl.when(market == m)
+        def _():
+            user_push(m).start()
+            for here, there in firsts(m):
                 there.start()
             for q in range(AHEAD):
-                for cp in pieces(k, q)[1::2]:
+                for cp in pieces(m, q)[1::2]:
                     cp.start()
 
-    for k in range(2):
-        @pl.when(core == k)
-        def _():
-            user_push(k).wait_recv()
-            users[1 - k] = users_in[...].T
+    user_push(0).wait_recv()
+    users[1 - core] = users_in[...].T
 
     def ready(role, j):
         for kind, buf in ((0, rates), (1, masks)):
@@ -141,18 +138,14 @@
         def _(n):
             sweep(users.at[role], items.at[s], rates.at[role, j], flags.at[role], step_u, step_v)
 
-    @pl.when(core == 1)
-    def _():
-        pl.delay(STAGGER)
-
     @pl.loop(0, stages + 1)
     def _(s):
         j = lax.rem(base + s, shards)
 
-        for k in range(2):
-            @pl.when(jnp.logical_and(core == k, s + AHEAD < shards))
+        for m in range(2):
+            @pl.when(jnp.logical_and(market == m, s + AHEAD < shards))
             def _():
-                for cp in pieces(k, s + AHEAD):
+                for cp in pieces(m, s + AHEAD):
                     cp.start()
 
         @pl.when(s < shards)
@@ -187,43 +180,49 @@
         def _():
             home(s, base - 1).start()
 
-    for k in range(2):
-        @pl.when(core == k)
-        def _():
-            user_home(k).start()
-            (ua_o, ub_o)[k][...] = users[k].T
+    user_home().start()
+    for m in range(2):
+        @pl.when(market == m)
+        def _():
+            (ua_o, ub_o)[m][...] = users[core].T
 
     @pl.when(core == 1)
     def _():
         home(stages, base).start()
 
-    def outs(k):
-        got = []
-        for m in range(2):
-            src = items.at[stages] if (k == 0 and m == 0) else last_items.at[m]
-            for c in range(chunks):
-                got.append(pltpu.make_async_copy(src.at[c], (va_o, vb_o)[m].at[:, pl.ds(c * CHUNK, CHUNK)], out_sem.at[m, c]))
-        return got
-
-    for k in range(2):
-        @pl.when(core == k)
-        def _():
-            for m in range(2):
-                if k or m:
-                    pltpu.make_async_copy(last_items.at[m], last_items.at[m], last_sem.at[m]).wait()
-            for cp in outs(k):
+    def outs(src, m):
+        return [pltpu.make_async_copy(src.at[c], (va_o, vb_o)[m].at[:, pl.ds(c * CHUNK, CHUNK)], out_sem.at[m, c])
+                for c in range(chunks)]
+
+    for m in range(2):
+        mine = jnp.logical_and(core == 0, market == m)
+
+        @pl.when(mine)
+        def _():
+            for cp in outs(items.at[stages], m):
                 cp.start()
-            user_home(k).wait()
-            (ua_o, ub_o)[1 - k][...] = users_out[...].T
-            for cp in outs(k):
-                cp.wait()
-            user_push(k).wait_send()
-            pltpu.make_async_copy(items.at[k], items.at[k], last_sem.at[2]).wait()
-
-            @pl.loop(0, shards)
-            def _(q):
-                for cp in pieces(k, q)[1::2]:
-                    cp.wait_send()
+
+        @pl.when(jnp.logical_not(mine))
+        def _():
+            pltpu.make_async_copy(last_items.at[m], last_items.at[m], last_sem.at[m]).wait()
+            for cp in outs(last_items.at[m], m):
+                cp.start()
+
+    user_home().wait()
+    for m in range(2):
+        @pl.when(market == m)
+        def _():
+            (ua_o, ub_o)[1 - m][...] = users_out[...].T
+    for m in range(2):
+        for cp in outs(last_items.at[m], m):
+            cp.wait()
+    user_push(0).wait_send()
+    pltpu.make_async_copy(items.at[core], items.at[core], last_sem.at[2]).wait()
+
+    @pl.loop(0, shards)
+    def _(j):
+        for kind, buf in ((0, rates), (1, masks)):
+            pltpu.make_async_copy(buf.at[core, j], buf.at[core, j], push_sem.at[kind, j]).wait()
 
     @pl.loop(0, stages)
     def _(s):

time: 137 us -> 135 us (0.985)
  Pallas kernels: 136 us -> 133 us
    pallas_call x1, Pallas kernels: 134 us -> 132 us  [device_body(): pl.pallas_call(functools.partial(kernel, shards, step_u, step_v), out_sha...]
where the time goes in v6:
time: 135 us; the launch traced here: 134 us
  Pallas kernels  133 us (99%)
    pallas_call x1, Pallas kernels, device_body(): pl.pallas_call(functools.partial(kernel, shards, step_u, step_v), out_sha...  132 us

profile of v6, /device:TPU:0, one launch (start us, length us, event | category | flops | bytes accessed | tf_op | source)
XLA Modules:
  0.0 134.0 jit_solution(6069246139065711806)
XLA Ops:
  0.6 131.7 %sweep_ring.1 = (f32[32,64]{1,0:T(8,128)}, f32[32,1024]{1,0:T(8,128)}, f32[32,64]{1,0:T(8,128)}, f32[32,1024]{1,0:T(8,128)}) custom-call(f32[64,16384]{1,0:T(8,128)} %ra.1, s32[64,16384]{1,0:T(8,128)} %ma.1, f32[32,64]{1,0:T(8,128)} %bitcast.10, f32[32,1024]{1,0:T(8,128)} %bitcast.8, f32[64,16384]{1,0:T(8,128)} %rb.1, s32[64,16384]{1,0:T(8,128)} %mb.1, ...), custom_call_target="tpu_custom_call" | custom-call | tf_op jit(solution)/shard_map/sweep_ring/pallas_call | solution.py:261
  132.3 1.7 %place.1 = (f32[32,64]{1,0:T(8,128)}, f32[32,1024]{1,0:T(8,128)}, f32[32,64]{1,0:T(8,128)}, f32[32,1024]{1,0:T(8,128)}) custom-call(f32[32,64]{1,0:T(8,128)} %get-tuple-element.12.ua, f32[32,1024]{1,0:T(8,128)} %get-tuple-element.13.va, f32[32,64]{1,0:T(8,128)} %get-tuple-element.14.ub, f32[32,1024]{1,0:T(8,128)} %get-tuple-element.15.vb), custom_call_target="tpu_custom_call" | custom-call | tf_op jit(solution)/shard_map/place/pallas_call | solution.py:287

commit v7 on v6

--- a/solution.py
+++ b/solution.py
@@ -12,6 +12,7 @@
 WEIGHT_DECAY = 0.05
 CHUNK = 256
 AHEAD = 3
+STAGGER = 1400
 MESH = pl.DeviceIdType.MESH
 
 
@@ -137,6 +138,10 @@
         @pl.loop(0, SWEEP_STEPS)
         def _(n):
             sweep(users.at[role], items.at[s], rates.at[role, j], flags.at[role], step_u, step_v)
+
+    @pl.when(market == 1)
+    def _():
+        pl.delay(STAGGER)
 
     @pl.loop(0, stages + 1)
     def _(s):

time: 135 us -> 135 us (level)
  the two profiles are of different devices: /device:TPU:0 before, /device:TPU:7 now
where the time goes in v7:
time: 135 us
  Pallas kernels  134 us (99%)
    pallas_call x1, Pallas kernels, device_body(): pl.pallas_call(functools.partial(kernel, shards, step_u, step_v), out_sha...  132 us

profile of v7, /device:TPU:7, one launch (start us, length us, event | category | flops | bytes accessed | tf_op | source)
XLA Modules:
  0.0 134.5 jit_solution(5656333789537406641)
XLA Ops:
  0.6 132.1 %sweep_ring.1 = (f32[32,64]{1,0:T(8,128)}, f32[32,1024]{1,0:T(8,128)}, f32[32,64]{1,0:T(8,128)}, f32[32,1024]{1,0:T(8,128)}) custom-call(f32[64,16384]{1,0:T(8,128)} %ra.1, s32[64,16384]{1,0:T(8,128)} %ma.1, f32[32,64]{1,0:T(8,128)} %bitcast.10, f32[32,1024]{1,0:T(8,128)} %bitcast.8, f32[64,16384]{1,0:T(8,128)} %rb.1, s32[64,16384]{1,0:T(8,128)} %mb.1, ...), custom_call_target="tpu_custom_call" | custom-call | tf_op jit(solution)/shard_map/sweep_ring/pallas_call | solution.py:266
  132.8 1.7 %place.1 = (f32[32,64]{1,0:T(8,128)}, f32[32,1024]{1,0:T(8,128)}, f32[32,64]{1,0:T(8,128)}, f32[32,1024]{1,0:T(8,128)}) custom-call(f32[32,64]{1,0:T(8,128)} %get-tuple-element.12.ua, f32[32,1024]{1,0:T(8,128)} %get-tuple-element.13.va, f32[32,64]{1,0:T(8,128)} %get-tuple-element.14.ub, f32[32,1024]{1,0:T(8,128)} %get-tuple-element.15.vb), custom_call_target="tpu_custom_call" | custom-call | tf_op jit(solution)/shard_map/place/pallas_call | solution.py:292

commit v8 on v6

--- a/solution.py
+++ b/solution.py
@@ -12,6 +12,7 @@
 WEIGHT_DECAY = 0.05
 CHUNK = 256
 AHEAD = 3
+STAGGER = 1400
 MESH = pl.DeviceIdType.MESH
 
 
@@ -134,8 +135,7 @@
             pltpu.make_async_copy(buf.at[role, j], buf.at[role, j], load_sem.at[kind, role, j]).wait()
 
     def visit(role, s, j):
-        @pl.loop(0, SWEEP_STEPS)
-        def _(n):
+        for _ in range(SWEEP_STEPS):
             sweep(users.at[role], items.at[s], rates.at[role, j], flags.at[role], step_u, step_v)
 
     @pl.loop(0, stages + 1)
@@ -163,6 +163,10 @@
             flags[1] = masks[1, j].astype(jnp.float32).astype(jnp.bfloat16)
 
         landed(s).wait()
+
+        @pl.when(jnp.logical_and(s == 0, market == 1))
+        def _():
+            pl.delay(STAGGER)
 
         @pl.when(s > 0)
         def _():

time: 135 us -> 135 us (level)
  no operation moved by 1% of the time
where the time goes in v8:
time: 135 us; the launch traced here: 134 us
  Pallas kernels  134 us (99%)
    pallas_call x1, Pallas kernels, device_body(): pl.pallas_call(functools.partial(kernel, shards, step_u, step_v), out_sha...  132 us

profile of v8, /device:TPU:0, one launch (start us, length us, event | category | flops | bytes accessed | tf_op | source)
XLA Modules:
  0.0 134.1 jit_solution(946024646216479612)
XLA Ops:
  0.6 131.8 %sweep_ring.1 = (f32[32,64]{1,0:T(8,128)}, f32[32,1024]{1,0:T(8,128)}, f32[32,64]{1,0:T(8,128)}, f32[32,1024]{1,0:T(8,128)}) custom-call(f32[64,16384]{1,0:T(8,128)} %ra.1, s32[64,16384]{1,0:T(8,128)} %ma.1, f32[32,64]{1,0:T(8,128)} %bitcast.10, f32[32,1024]{1,0:T(8,128)} %bitcast.8, f32[64,16384]{1,0:T(8,128)} %rb.1, s32[64,16384]{1,0:T(8,128)} %mb.1, ...), custom_call_target="tpu_custom_call" | custom-call | tf_op jit(solution)/shard_map/sweep_ring/pallas_call | solution.py:265
  132.4 1.7 %place.1 = (f32[32,64]{1,0:T(8,128)}, f32[32,1024]{1,0:T(8,128)}, f32[32,64]{1,0:T(8,128)}, f32[32,1024]{1,0:T(8,128)}) custom-call(f32[32,64]{1,0:T(8,128)} %get-tuple-element.12.ua, f32[32,1024]{1,0:T(8,128)} %get-tuple-element.13.va, f32[32,64]{1,0:T(8,128)} %get-tuple-element.14.ub, f32[32,1024]{1,0:T(8,128)} %get-tuple-element.15.vb), custom_call_target="tpu_custom_call" | custom-call | tf_op jit(solution)/shard_map/place/pallas_call | solution.py:291

commit v9 on v8

--- a/solution.py
+++ b/solution.py
@@ -13,6 +13,7 @@
 CHUNK = 256
 AHEAD = 3
 STAGGER = 1400
+LINK = 750
 MESH = pl.DeviceIdType.MESH
 
 
@@ -39,7 +40,7 @@
 
 def kernel(shards, step_u, step_v, ra, ma, ua, va, rb, mb, ub, vb, ua_o, va_o, ub_o, vb_o,
            rates, masks, flags, items, last_items, users, users_in, users_out,
-           load_sem, push_sem, send_sem, recv_sem, last_sem, user_sem, out_sem):
+           load_sem, push_sem, send_sem, recv_sem, last_sem, user_sem, out_sem, go_sem):
     me = lax.axis_index("shard")
     core = lax.rem(me, 2)
     base = me - core
@@ -102,8 +103,13 @@
         return pltpu.make_async_copy(items.at[s], items.at[s], recv_sem.at[s])
 
     barrier = pltpu.get_barrier_semaphore()
-    for other in (base - 2, base - 1, peer, base + 2, base + 3):
-        pl.semaphore_signal(barrier, inc=1, device_id=dev(other), device_id_type=MESH)
+    chip, chips = base // 2, shards // 2
+    near = ((peer, chip >= 0), (base - 2, chip >= 1), (base - 1, chip >= 1), (base + 2, chip < chips - 1),
+            (base + 3, chip < chips - 1), (me - 4, chip >= 2), (me + 4, chip < chips - 2))
+    for other, there in near:
+        @pl.when(there)
+        def _():
+            pl.semaphore_signal(barrier, inc=1, device_id=dev(other), device_id_type=MESH)
 
     for m in range(2):
         @pl.when(market == m)
@@ -115,7 +121,7 @@
                     cp.start()
             users[core] = own(m)[2][...].T
 
-    pl.semaphore_wait(barrier, 5)
+    pl.semaphore_wait(barrier, sum(there.astype(jnp.int32) for _, there in near))
 
     for m in range(2):
         @pl.when(market == m)
@@ -130,6 +136,33 @@
     user_push(0).wait_recv()
     users[1 - core] = users_in[...].T
 
+    even = lax.rem(chip, 2) == 0
+
+    @pl.when(chip < chips - 1)
+    def _():
+        pl.semaphore_wait(go_sem, 1)
+
+    @pl.when(jnp.logical_not(even))
+    def _():
+        pl.semaphore_signal(go_sem, inc=1, device_id=dev(me - 2), device_id_type=MESH)
+
+    @pl.when(jnp.logical_and(jnp.logical_not(even), chip >= 2))
+    def _():
+        pl.semaphore_signal(go_sem, inc=1, device_id=dev(me - 4), device_id_type=MESH)
+
+    def hold():
+        ahead = chip // 2 + lax.rem(chip, 2)
+        for n in range(1, chips // 2 + 1):
+            @pl.when(ahead == n)
+            def _():
+                pl.delay(n * LINK)
+
+        @pl.when(market == 1)
+        def _():
+            pl.delay(STAGGER)
+
+    hold()
+
     def ready(role, j):
         for kind, buf in ((0, rates), (1, masks)):
             pltpu.make_async_copy(buf.at[role, j], buf.at[role, j], load_sem.at[kind, role, j]).wait()
@@ -163,10 +196,6 @@
             flags[1] = masks[1, j].astype(jnp.float32).astype(jnp.bfloat16)
 
         landed(s).wait()
-
-        @pl.when(jnp.logical_and(s == 0, market == 1))
-        def _():
-            pl.delay(STAGGER)
 
         @pl.when(s > 0)
         def _():
@@ -283,6 +312,7 @@
                 pltpu.SemaphoreType.DMA((3,)),
                 pltpu.SemaphoreType.DMA((4,)),
                 pltpu.SemaphoreType.DMA((2, chunks)),
+                pltpu.SemaphoreType.REGULAR,
             ],
             compiler_params=pltpu.CompilerParams(
                 collective_id=0, has_side_effects=True, vmem_limit_bytes=60 * 1024 * 1024),

time: 135 us -> 139 us (1.030)
  the two profiles are of different devices: /device:TPU:0 before, /device:TPU:3 now
where the time goes in v9:
time: 139 us
  Pallas kernels  138 us (99%)
    pallas_call x1, Pallas kernels, device_body(): pl.pallas_call(functools.partial(kernel, shards, step_u, step_v), out_sha...  136 us

profile of v9, /device:TPU:3, one launch (start us, length us, event | category | flops | bytes accessed | tf_op | source)
XLA Modules:
  0.0 138.7 jit_solution(9875137398877259401)
XLA Ops:
  0.6 136.3 %sweep_ring.1 = (f32[32,64]{1,0:T(8,128)}, f32[32,1024]{1,0:T(8,128)}, f32[32,64]{1,0:T(8,128)}, f32[32,1024]{1,0:T(8,128)}) custom-call(f32[64,16384]{1,0:T(8,128)} %ra.1, s32[64,16384]{1,0:T(8,128)} %ma.1, f32[32,64]{1,0:T(8,128)} %bitcast.10, f32[32,1024]{1,0:T(8,128)} %bitcast.8, f32[64,16384]{1,0:T(8,128)} %rb.1, s32[64,16384]{1,0:T(8,128)} %mb.1, ...), custom_call_target="tpu_custom_call" | custom-call | tf_op jit(solution)/shard_map/sweep_ring/pallas_call | solution.py:294
  137.0 1.7 %place.1 = (f32[32,64]{1,0:T(8,128)}, f32[32,1024]{1,0:T(8,128)}, f32[32,64]{1,0:T(8,128)}, f32[32,1024]{1,0:T(8,128)}) custom-call(f32[32,64]{1,0:T(8,128)} %get-tuple-element.12.ua, f32[32,1024]{1,0:T(8,128)} %get-tuple-element.13.va, f32[32,64]{1,0:T(8,128)} %get-tuple-element.14.ub, f32[32,1024]{1,0:T(8,128)} %get-tuple-element.15.vb), custom_call_target="tpu_custom_call" | custom-call | tf_op jit(solution)/shard_map/place/pallas_call | solution.py:321

commit v10 on v9

--- a/solution.py
+++ b/solution.py
@@ -12,8 +12,6 @@
 WEIGHT_DECAY = 0.05
 CHUNK = 256
 AHEAD = 3
-STAGGER = 1400
-LINK = 750
 MESH = pl.DeviceIdType.MESH
 
 
@@ -138,30 +136,19 @@
 
     even = lax.rem(chip, 2) == 0
 
-    @pl.when(chip < chips - 1)
+    hears = jnp.logical_or(chip == 0, jnp.logical_and(jnp.logical_not(even), chip < chips - 1))
+
+    @pl.when(hears)
     def _():
         pl.semaphore_wait(go_sem, 1)
 
-    @pl.when(jnp.logical_not(even))
+    @pl.when(chip == 1)
     def _():
         pl.semaphore_signal(go_sem, inc=1, device_id=dev(me - 2), device_id_type=MESH)
 
     @pl.when(jnp.logical_and(jnp.logical_not(even), chip >= 2))
     def _():
         pl.semaphore_signal(go_sem, inc=1, device_id=dev(me - 4), device_id_type=MESH)
-
-    def hold():
-        ahead = chip // 2 + lax.rem(chip, 2)
-        for n in range(1, chips // 2 + 1):
-            @pl.when(ahead == n)
-            def _():
-                pl.delay(n * LINK)
-
-        @pl.when(market == 1)
-        def _():
-            pl.delay(STAGGER)
-
-    hold()
 
     def ready(role, j):
         for kind, buf in ((0, rates), (1, masks)):

time: 139 us -> 136 us (0.978)
  the two profiles are of different devices: /device:TPU:3 before, /device:TPU:0 now
where the time goes in v10:
time: 136 us; the launch traced here: 135 us
  Pallas kernels  134 us (99%)
    pallas_call x1, Pallas kernels, device_body(): pl.pallas_call(functools.partial(kernel, shards, step_u, step_v), out_sha...  132 us

profile of v10, /device:TPU:0, one launch (start us, length us, event | category | flops | bytes accessed | tf_op | source)
XLA Modules:
  0.0 134.5 jit_solution(4097587199352595884)
XLA Ops:
  0.6 132.2 %sweep_ring.1 = (f32[32,64]{1,0:T(8,128)}, f32[32,1024]{1,0:T(8,128)}, f32[32,64]{1,0:T(8,128)}, f32[32,1024]{1,0:T(8,128)}) custom-call(f32[64,16384]{1,0:T(8,128)} %ra.1, s32[64,16384]{1,0:T(8,128)} %ma.1, f32[32,64]{1,0:T(8,128)} %bitcast.10, f32[32,1024]{1,0:T(8,128)} %bitcast.8, f32[64,16384]{1,0:T(8,128)} %rb.1, s32[64,16384]{1,0:T(8,128)} %mb.1, ...), custom_call_target="tpu_custom_call" | custom-call | tf_op jit(solution)/shard_map/sweep_ring/pallas_call | solution.py:281
  132.8 1.7 %place.1 = (f32[32,64]{1,0:T(8,128)}, f32[32,1024]{1,0:T(8,128)}, f32[32,64]{1,0:T(8,128)}, f32[32,1024]{1,0:T(8,128)}) custom-call(f32[32,64]{1,0:T(8,128)} %get-tuple-element.12.ua, f32[32,1024]{1,0:T(8,128)} %get-tuple-element.13.va, f32[32,64]{1,0:T(8,128)} %get-tuple-element.14.ub, f32[32,1024]{1,0:T(8,128)} %get-tuple-element.15.vb), custom_call_target="tpu_custom_call" | custom-call | tf_op jit(solution)/shard_map/place/pallas_call | solution.py:308

commit v11 on v2

--- a/solution.py
+++ b/solution.py
@@ -15,20 +15,23 @@
 
 
 def sweep(u_ref, v_ref, rate_ref, flag_ref, step_u, step_v):
+    chunks = range(v_ref.shape[0])
+    f32, bf16 = jnp.float32, jnp.bfloat16
     user = u_ref[...]
-    user_low = user.astype(jnp.bfloat16)
-    user_low_t = user.T.astype(jnp.bfloat16)
-    grad_u = None
-    for c in range(v_ref.shape[0]):
+    user_low = user.astype(bf16)
+    user_low_t = user.T.astype(bf16)
+    item_low = [v_ref[c].astype(bf16) for c in chunks]
+    approx = [jnp.dot(user_low, item_low[c], preferred_element_type=f32) for c in chunks]
+    err_low = []
+    for c in chunks:
         cols = pl.ds(c * CHUNK, CHUNK)
+        err_low.append((approx[c] - rate_ref[:, cols]).astype(bf16) * flag_ref[:, cols])
+    part = [lax.dot_general(err_low[c], item_low[c], (((1,), (1,)), ((), ())), preferred_element_type=f32) for c in chunks]
+    grad_v = [jnp.dot(user_low_t, err_low[c], preferred_element_type=f32) for c in chunks]
+    for c in chunks:
         item = v_ref[c]
-        item_low = item.astype(jnp.bfloat16)
-        approx = jnp.dot(user_low, item_low, preferred_element_type=jnp.float32)
-        err_low = (approx - rate_ref[:, cols]).astype(jnp.bfloat16) * flag_ref[:, cols]
-        part = lax.dot_general(err_low, item_low, (((1,), (1,)), ((), ())), preferred_element_type=jnp.float32)
-        grad_u = part if grad_u is None else grad_u + part
-        grad_v = jnp.dot(user_low_t, err_low, preferred_element_type=jnp.float32)
-        v_ref[c] = item - step_v * (grad_v + WEIGHT_DECAY * item)
+        v_ref[c] = item - step_v * (grad_v[c] + WEIGHT_DECAY * item)
+    grad_u = (part[0] + part[1]) + (part[2] + part[3])
     u_ref[...] = user - step_u * (grad_u + WEIGHT_DECAY * user)
 
 
@@ -91,13 +94,12 @@
                 for cp in loads(m, t):
                     cp.wait()
             flags[m] = masks[m, j].astype(jnp.float32).astype(jnp.bfloat16)
-
+        for m in range(2):
             @pl.when(t > 0)
             def _():
                 hop(m, t - 1).wait_recv()
 
-            @pl.loop(0, SWEEP_STEPS)
-            def _(s):
+            for _ in range(SWEEP_STEPS):
                 sweep(users.at[m], items.at[m, t], rates.at[m, j], flags.at[m], step_u, step_v)
             hop(m, t).start()
 
@@ -115,6 +117,15 @@
     def _(t):
         for m in range(2):
             hop(m, t).wait_send()
+
+
+def place(ua, va, ub, vb, ua_o, va_o, ub_o, vb_o, sem):
+    copies = [pltpu.make_async_copy(src, dst, sem.at[i])
+              for i, (src, dst) in enumerate(((ua, ua_o), (va, va_o), (ub, ub_o), (vb, vb_o)))]
+    for cp in copies:
+        cp.start()
+    for cp in copies:
+        cp.wait()
 
 
 def solution(mesh):
@@ -137,7 +148,7 @@
             functools.partial(kernel, shards, step_u, step_v),
             out_shape=(ut, vt, ut, vt),
             in_specs=[hbm, hbm, vmem, hbm] * 2,
-            out_specs=[vmem, hbm] * 2,
+            out_specs=[vmem] * 4,
             scratch_shapes=[
                 pltpu.VMEM((2, shards, users_dev, block), f32),
                 pltpu.VMEM((2, shards, users_dev, block), jnp.int32),
@@ -151,9 +162,18 @@
                 pltpu.SemaphoreType.DMA((2, chunks)),
             ],
             compiler_params=pltpu.CompilerParams(
-                collective_id=0, has_side_effects=True, vmem_limit_bytes=48 * 1024 * 1024),
+                collective_id=0, has_side_effects=True, vmem_limit_bytes=60 * 1024 * 1024),
             name="sweep_ring",
         )(ratings_a, mask_a, users_a.T, items_a.T, ratings_b, mask_b, users_b.T, items_b.T)
+        outs = pl.pallas_call(
+            place,
+            out_shape=(ut, vt, ut, vt),
+            in_specs=[vmem] * 4,
+            out_specs=[pl.BlockSpec(memory_space=pl.ANY)] * 4,
+            scratch_shapes=[pltpu.SemaphoreType.DMA((4,))],
+            compiler_params=pltpu.CompilerParams(vmem_limit_bytes=60 * 1024 * 1024),
+            name="place",
+        )(*outs)
         return tuple(o.T for o in outs)
 
     return jax.shard_map(device_body, mesh=mesh, in_specs=(row_spec,) * 8, out_specs=(row_spec,) * 4, check_vma=False)

time: 197 us -> 135 us (0.69)
  Pallas kernels: 188 us -> 133 us
  local copies, waits for them, and re-layouts: 7.94 us -> 0 us
    pallas_call x1, Pallas kernels: 188 us -> 132 us  [device_body(): pl.pallas_call(functools.partial(kernel, shards, step_u, step_v), out_sha...]
    unnamed x14 -> x0, local copies, waits for them, and re-layouts: 7.94 us -> none
where the time goes in v11:
time: 135 us; the launch traced here: 134 us
  Pallas kernels  133 us (99%)
    pallas_call x1, Pallas kernels, device_body(): pl.pallas_call(functools.partial(kernel, shards, step_u, step_v), out_sha...  132 us

profile of v11, /device:TPU:0, one launch (start us, length us, event | category | flops | bytes accessed | tf_op | source)
XLA Modules:
  0.0 134.1 jit_solution(14419954958592703340)
XLA Ops:
  0.6 131.7 %sweep_ring.1 = (f32[32,64]{1,0:T(8,128)}, f32[32,1024]{1,0:T(8,128)}, f32[32,64]{1,0:T(8,128)}, f32[32,1024]{1,0:T(8,128)}) custom-call(f32[64,16384]{1,0:T(8,128)} %ra.1, s32[64,16384]{1,0:T(8,128)} %ma.1, f32[32,64]{1,0:T(8,128)} %bitcast.10, f32[32,1024]{1,0:T(8,128)} %bitcast.8, f32[64,16384]{1,0:T(8,128)} %rb.1, s32[64,16384]{1,0:T(8,128)} %mb.1, ...), custom_call_target="tpu_custom_call" | custom-call | tf_op jit(solution)/shard_map/sweep_ring/pallas_call | solution.py:147
  132.3 1.7 %place.1 = (f32[32,64]{1,0:T(8,128)}, f32[32,1024]{1,0:T(8,128)}, f32[32,64]{1,0:T(8,128)}, f32[32,1024]{1,0:T(8,128)}) custom-call(f32[32,64]{1,0:T(8,128)} %get-tuple-element.12.ua, f32[32,1024]{1,0:T(8,128)} %get-tuple-element.13.va, f32[32,64]{1,0:T(8,128)} %get-tuple-element.14.ub, f32[32,1024]{1,0:T(8,128)} %get-tuple-element.15.vb), custom_call_target="tpu_custom_call" | custom-call | tf_op jit(solution)/shard_map/place/pallas_call | solution.py:168

commit v12 on v11

--- a/solution.py
+++ b/solution.py
@@ -36,7 +36,7 @@
 
 
 def kernel(shards, step_u, step_v, ra, ma, ua, va, rb, mb, ub, vb, ua_o, va_o, ub_o, vb_o,
-           rates, masks, flags, items, users, load_sem, first_sem, send_sem, recv_sem, out_sem):
+           rates, masks, flags, items, users, users_t, load_sem, first_sem, send_sem, recv_sem, out_sem, user_sem):
     me = lax.axis_index("shard")
     left = lax.rem(me + shards - 1, shards)
     right = lax.rem(me + 1, shards)
@@ -62,9 +62,16 @@
             src_ref=items.at[m, t], dst_ref=items.at[m, t + 1], send_sem=send_sem.at[m, t],
             recv_sem=recv_sem.at[m, t + 1], device_id={"shard": left}, device_id_type=MESH)
 
+    def user_in(m):
+        return pltpu.make_async_copy((ua, ub)[m], users_t.at[m], user_sem.at[m])
+
+    def user_out(m):
+        return pltpu.make_async_copy(users_t.at[m], (ua_o, ub_o)[m], user_sem.at[m])
+
     for m in range(2):
         for c in range(chunks):
             first(m, c).start()
+        user_in(m).start()
         for cp in loads(m, 0):
             cp.start()
 
@@ -78,12 +85,11 @@
             for cp in loads(m, t):
                 cp.start()
 
-    users[0] = ua[...].T
-    users[1] = ub[...].T
     for m in range(2):
+        user_in(m).wait()
+        users[m] = users_t[m].T
         for c in range(chunks):
             first(m, c).wait()
-    pl.semaphore_wait(barrier, 2)
 
     @pl.loop(0, stages)
     def _(t):
@@ -101,17 +107,23 @@
 
             for _ in range(SWEEP_STEPS):
                 sweep(users.at[m], items.at[m, t], rates.at[m, j], flags.at[m], step_u, step_v)
+            if m == 0:
+                @pl.when(t == 0)
+                def _():
+                    pl.semaphore_wait(barrier, 2)
             hop(m, t).start()
 
-    ua_o[...] = users[0].T
-    ub_o[...] = users[1].T
     for m in range(2):
+        users_t[m] = users[m].T
+    for m in range(2):
+        user_out(m).start()
         hop(m, stages - 1).wait_recv()
         for c in range(chunks):
             last(m, c).start()
     for m in range(2):
         for c in range(chunks):
             last(m, c).wait()
+        user_out(m).wait()
 
     @pl.loop(0, stages)
     def _(t):
@@ -147,19 +159,21 @@
         outs = pl.pallas_call(
             functools.partial(kernel, shards, step_u, step_v),
             out_shape=(ut, vt, ut, vt),
-            in_specs=[hbm, hbm, vmem, hbm] * 2,
-            out_specs=[vmem] * 4,
+            in_specs=[hbm] * 8,
+            out_specs=[hbm] * 4,
             scratch_shapes=[
                 pltpu.VMEM((2, shards, users_dev, block), f32),
                 pltpu.VMEM((2, shards, users_dev, block), jnp.int32),
                 pltpu.VMEM((2, users_dev, block), jnp.bfloat16),
                 pltpu.VMEM((2, stages + 1, chunks, rank, CHUNK), f32),
                 pltpu.VMEM((2, users_dev, rank), f32),
+                pltpu.VMEM((2, rank, users_dev), f32),
                 pltpu.SemaphoreType.DMA((2, 2, shards)),
                 pltpu.SemaphoreType.DMA((2, chunks)),
                 pltpu.SemaphoreType.DMA((2, stages)),
                 pltpu.SemaphoreType.DMA((2, stages + 1)),
                 pltpu.SemaphoreType.DMA((2, chunks)),
+                pltpu.SemaphoreType.DMA((2,)),
             ],
             compiler_params=pltpu.CompilerParams(
                 collective_id=0, has_side_effects=True, vmem_limit_bytes=60 * 1024 * 1024),

time: 135 us -> 132 us (0.978)
  Pallas kernels: 133 us -> 131 us
    pallas_call x1, Pallas kernels: 132 us -> 130 us  [device_body(): pl.pallas_call(functools.partial(kernel, shards, step_u, step_v), out_sha...]
where the time goes in v12:
time: 132 us
  Pallas kernels  131 us (99%)
    pallas_call x1, Pallas kernels, device_body(): pl.pallas_call(functools.partial(kernel, shards, step_u, step_v), out_sha...  130 us

profile of v12, /device:TPU:0, one launch (start us, length us, event | category | flops | bytes accessed | tf_op | source)
XLA Modules:
  0.0 132.0 jit_solution(6817692193073679959)
XLA Ops:
  0.6 129.6 %sweep_ring.1 = (f32[32,64]{1,0:T(8,128)}, f32[32,1024]{1,0:T(8,128)}, f32[32,64]{1,0:T(8,128)}, f32[32,1024]{1,0:T(8,128)}) custom-call(f32[64,16384]{1,0:T(8,128)} %ra.1, s32[64,16384]{1,0:T(8,128)} %ma.1, f32[32,64]{1,0:T(8,128)} %bitcast.10, f32[32,1024]{1,0:T(8,128)} %bitcast.8, f32[64,16384]{1,0:T(8,128)} %rb.1, s32[64,16384]{1,0:T(8,128)} %mb.1, ...), custom_call_target="tpu_custom_call" | custom-call | tf_op jit(solution)/shard_map/sweep_ring/pallas_call | solution.py:159
  130.3 1.7 %place.1 = (f32[32,64]{1,0:T(8,128)}, f32[32,1024]{1,0:T(8,128)}, f32[32,64]{1,0:T(8,128)}, f32[32,1024]{1,0:T(8,128)}) custom-call(f32[32,64]{1,0:T(8,128)} %get-tuple-element.12.ua, f32[32,1024]{1,0:T(8,128)} %get-tuple-element.13.va, f32[32,64]{1,0:T(8,128)} %get-tuple-element.14.ub, f32[32,1024]{1,0:T(8,128)} %get-tuple-element.15.vb), custom_call_target="tpu_custom_call" | custom-call | tf_op jit(solution)/shard_map/place/pallas_call | solution.py:182

commit v13 on v10

--- a/solution.py
+++ b/solution.py
@@ -12,6 +12,7 @@
 WEIGHT_DECAY = 0.05
 CHUNK = 256
 AHEAD = 3
+STAGGER = 1400
 MESH = pl.DeviceIdType.MESH
 
 
@@ -37,8 +38,8 @@
 
 
 def kernel(shards, step_u, step_v, ra, ma, ua, va, rb, mb, ub, vb, ua_o, va_o, ub_o, vb_o,
-           rates, masks, flags, items, last_items, users, users_in, users_out,
-           load_sem, push_sem, send_sem, recv_sem, last_sem, user_sem, out_sem, go_sem):
+           rates, masks, flags, items, last_items, users, users_t, users_in, users_out,
+           load_sem, push_sem, send_sem, recv_sem, last_sem, user_sem, out_sem, go_sem, pair_sem):
     me = lax.axis_index("shard")
     core = lax.rem(me, 2)
     base = me - core
@@ -117,7 +118,7 @@
             for q in range(AHEAD):
                 for cp in pieces(m, q)[0::2]:
                     cp.start()
-            users[core] = own(m)[2][...].T
+            pltpu.make_async_copy(own(m)[2], users_t, user_sem.at[4]).start()
 
     pl.semaphore_wait(barrier, sum(there.astype(jnp.int32) for _, there in near))
 
@@ -131,6 +132,8 @@
                 for cp in pieces(m, q)[1::2]:
                     cp.start()
 
+    pltpu.make_async_copy(users_t, users_t, user_sem.at[4]).wait()
+    users[core] = users_t[...].T
     user_push(0).wait_recv()
     users[1 - core] = users_in[...].T
 
@@ -184,6 +187,15 @@
 
         landed(s).wait()
 
+        @pl.when(s == 0)
+        def _():
+            pl.semaphore_signal(pair_sem, inc=1, device_id=dev(peer), device_id_type=MESH)
+            pl.semaphore_wait(pair_sem, 1)
+
+            @pl.when(market == 1)
+            def _():
+                pl.delay(STAGGER)
+
         @pl.when(s > 0)
         def _():
             visit(1, s, j)
@@ -201,10 +213,11 @@
             home(s, base - 1).start()
 
     user_home().start()
+    users_t[...] = users[core].T
     for m in range(2):
         @pl.when(market == m)
         def _():
-            (ua_o, ub_o)[m][...] = users[core].T
+            pltpu.make_async_copy(users_t, (ua_o, ub_o)[m], user_sem.at[5]).start()
 
     @pl.when(core == 1)
     def _():
@@ -229,10 +242,13 @@
                 cp.start()
 
     user_home().wait()
+    users_in[...] = users_out[...].T
     for m in range(2):
         @pl.when(market == m)
         def _():
-            (ua_o, ub_o)[1 - m][...] = users_out[...].T
+            pltpu.make_async_copy(users_in, (ua_o, ub_o)[1 - m], user_sem.at[6]).start()
+    pltpu.make_async_copy(users_t, users_t, user_sem.at[5]).wait()
+    pltpu.make_async_copy(users_in, users_in, user_sem.at[6]).wait()
     for m in range(2):
         for cp in outs(last_items.at[m], m):
             cp.wait()
@@ -281,8 +297,8 @@
         outs = pl.pallas_call(
             functools.partial(kernel, shards, step_u, step_v),
             out_shape=(ut, vt, ut, vt),
-            in_specs=[hbm, hbm, vmem, hbm] * 2,
-            out_specs=[vmem] * 4,
+            in_specs=[hbm] * 8,
+            out_specs=[hbm] * 4,
             scratch_shapes=[
                 pltpu.VMEM((2, shards, users_dev, block), f32),
                 pltpu.VMEM((2, shards, users_dev, block), jnp.int32),
@@ -291,14 +307,16 @@
                 pltpu.VMEM((2, chunks, rank, CHUNK), f32),
                 pltpu.VMEM((2, users_dev, rank), f32),
                 pltpu.VMEM((rank, users_dev), f32),
+                pltpu.VMEM((rank, users_dev), f32),
                 pltpu.VMEM((users_dev, rank), f32),
                 pltpu.SemaphoreType.DMA((2, 2, shards)),
                 pltpu.SemaphoreType.DMA((2, shards)),
                 pltpu.SemaphoreType.DMA((stages + 1,)),
                 pltpu.SemaphoreType.DMA((stages + 1,)),
                 pltpu.SemaphoreType.DMA((3,)),
-                pltpu.SemaphoreType.DMA((4,)),
+                pltpu.SemaphoreType.DMA((7,)),
                 pltpu.SemaphoreType.DMA((2, chunks)),
+                pltpu.SemaphoreType.REGULAR,
                 pltpu.SemaphoreType.REGULAR,
             ],
             compiler_params=pltpu.CompilerParams(

time: 136 us -> 135 us (level)
  Pallas kernels: 134 us -> 132 us
    pallas_call x1, Pallas kernels: 132 us -> 131 us  [device_body(): pl.pallas_call(functools.partial(kernel, shards, step_u, step_v), out_sha...]
where the time goes in v13:
time: 135 us; the launch traced here: 133 us
  Pallas kernels  132 us (98%)
    pallas_call x1, Pallas kernels, device_body(): pl.pallas_call(functools.partial(kernel, shards, step_u, step_v), out_sha...  131 us

profile of v13, /device:TPU:0, one launch (start us, length us, event | category | flops | bytes accessed | tf_op | source)
XLA Modules:
  0.0 133.1 jit_solution(12444281717482188572)
XLA Ops:
  0.6 130.7 %sweep_ring.1 = (f32[32,64]{1,0:T(8,128)}, f32[32,1024]{1,0:T(8,128)}, f32[32,64]{1,0:T(8,128)}, f32[32,1024]{1,0:T(8,128)}) custom-call(f32[64,16384]{1,0:T(8,128)} %ra.1, s32[64,16384]{1,0:T(8,128)} %ma.1, f32[32,64]{1,0:T(8,128)} %bitcast.10, f32[32,1024]{1,0:T(8,128)} %bitcast.8, f32[64,16384]{1,0:T(8,128)} %rb.1, s32[64,16384]{1,0:T(8,128)} %mb.1, ...), custom_call_target="tpu_custom_call" | custom-call | tf_op jit(solution)/shard_map/sweep_ring/pallas_call | solution.py:297
  131.3 1.7 %place.1 = (f32[32,64]{1,0:T(8,128)}, f32[32,1024]{1,0:T(8,128)}, f32[32,64]{1,0:T(8,128)}, f32[32,1024]{1,0:T(8,128)}) custom-call(f32[32,64]{1,0:T(8,128)} %get-tuple-element.12.ua, f32[32,1024]{1,0:T(8,128)} %get-tuple-element.13.va, f32[32,64]{1,0:T(8,128)} %get-tuple-element.14.ub, f32[32,1024]{1,0:T(8,128)} %get-tuple-element.15.vb), custom_call_target="tpu_custom_call" | custom-call | tf_op jit(solution)/shard_map/place/pallas_call | solution.py:326

commit v14 on v12

--- a/solution.py
+++ b/solution.py
@@ -11,6 +11,7 @@
 EPOCHS = 2
 WEIGHT_DECAY = 0.05
 CHUNK = 256
+AHEAD = 2
 MESH = pl.DeviceIdType.MESH
 
 
@@ -79,8 +80,7 @@
     for other in (left, right):
         pl.semaphore_signal(barrier, inc=1, device_id={"shard": other}, device_id_type=MESH)
 
-    @pl.loop(1, shards)
-    def _(t):
+    for t in range(1, AHEAD):
         for m in range(2):
             for cp in loads(m, t):
                 cp.start()
@@ -94,6 +94,12 @@
     @pl.loop(0, stages)
     def _(t):
         j = lax.rem(me + t, shards)
+
+        @pl.when(t + AHEAD < shards)
+        def _():
+            for m in range(2):
+                for cp in loads(m, t + AHEAD):
+                    cp.start()
         for m in range(2):
             @pl.when(t < shards)
             def _():
@@ -117,6 +123,13 @@
         users_t[m] = users[m].T
     for m in range(2):
         user_out(m).start()
+
+    @pl.loop(0, stages - 1)
+    def _(t):
+        for m in range(2):
+            hop(m, t).wait_send()
+
+    for m in range(2):
         hop(m, stages - 1).wait_recv()
         for c in range(chunks):
             last(m, c).start()
@@ -125,10 +138,8 @@
             last(m, c).wait()
         user_out(m).wait()
 
-    @pl.loop(0, stages)
-    def _(t):
-        for m in range(2):
-            hop(m, t).wait_send()
+    for m in range(2):
+        hop(m, stages - 1).wait_send()
 
 
 def place(ua, va, ub, vb, ua_o, va_o, ub_o, vb_o, sem):

time: 132 us -> 132 us (level)
  no operation moved by 1% of the time
where the time goes in v14:
time: 132 us
  Pallas kernels  131 us (99%)
    pallas_call x1, Pallas kernels, device_body(): pl.pallas_call(functools.partial(kernel, shards, step_u, step_v), out_sha...  129 us

profile of v14, /device:TPU:0, one launch (start us, length us, event | category | flops | bytes accessed | tf_op | source)
XLA Modules:
  0.0 131.8 jit_solution(8209723109945454948)
XLA Ops:
  0.6 129.4 %sweep_ring.1 = (f32[32,64]{1,0:T(8,128)}, f32[32,1024]{1,0:T(8,128)}, f32[32,64]{1,0:T(8,128)}, f32[32,1024]{1,0:T(8,128)}) custom-call(f32[64,16384]{1,0:T(8,128)} %ra.1, s32[64,16384]{1,0:T(8,128)} %ma.1, f32[32,64]{1,0:T(8,128)} %bitcast.10, f32[32,1024]{1,0:T(8,128)} %bitcast.8, f32[64,16384]{1,0:T(8,128)} %rb.1, s32[64,16384]{1,0:T(8,128)} %mb.1, ...), custom_call_target="tpu_custom_call" | custom-call | tf_op jit(solution)/shard_map/sweep_ring/pallas_call | solution.py:170
  130.1 1.7 %place.1 = (f32[32,64]{1,0:T(8,128)}, f32[32,1024]{1,0:T(8,128)}, f32[32,64]{1,0:T(8,128)}, f32[32,1024]{1,0:T(8,128)}) custom-call(f32[32,64]{1,0:T(8,128)} %get-tuple-element.12.ua, f32[32,1024]{1,0:T(8,128)} %get-tuple-element.13.va, f32[32,64]{1,0:T(8,128)} %get-tuple-element.14.ub, f32[32,1024]{1,0:T(8,128)} %get-tuple-element.15.vb), custom_call_target="tpu_custom_call" | custom-call | tf_op jit(solution)/shard_map/place/pallas_call | solution.py:193

commit v15 on v14

--- a/solution.py
+++ b/solution.py
@@ -142,12 +142,16 @@
         hop(m, stages - 1).wait_send()
 
 
-def place(ua, va, ub, vb, ua_o, va_o, ub_o, vb_o, sem):
-    copies = [pltpu.make_async_copy(src, dst, sem.at[i])
-              for i, (src, dst) in enumerate(((ua, ua_o), (va, va_o), (ub, ub_o), (vb, vb_o)))]
-    for cp in copies:
+def place(ua, va, ub, vb, ua_o, va_o, ub_o, vb_o, ua_t, va_t, ub_t, vb_t, sem):
+    route = ((ua, ua_t, ua_o), (va, va_t, va_o), (ub, ub_t, ub_o), (vb, vb_t, vb_o))
+    loads = [pltpu.make_async_copy(src, mid, sem.at[0, i]) for i, (src, mid, _) in enumerate(route)]
+    stores = [pltpu.make_async_copy(mid, dst, sem.at[1, i]) for i, (_, mid, dst) in enumerate(route)]
+    for cp in loads:
         cp.start()
-    for cp in copies:
+    for load, store in zip(loads, stores):
+        load.wait()
+        store.start()
+    for cp in stores:
         cp.wait()
 
 
@@ -163,7 +167,6 @@
         step_u = 0.5 * math.sqrt(rank) / (block + 2 * rank)
         step_v = 0.5 * math.sqrt(rank) / (users_dev + 2 * rank)
         hbm = pl.BlockSpec(memory_space=pltpu.HBM)
-        vmem = pl.BlockSpec(memory_space=pltpu.VMEM)
         f32 = jnp.float32
         ut = jax.ShapeDtypeStruct((rank, users_dev), f32)
         vt = jax.ShapeDtypeStruct((rank, block), f32)
@@ -193,9 +196,9 @@
         outs = pl.pallas_call(
             place,
             out_shape=(ut, vt, ut, vt),
-            in_specs=[vmem] * 4,
-            out_specs=[pl.BlockSpec(memory_space=pl.ANY)] * 4,
-            scratch_shapes=[pltpu.SemaphoreType.DMA((4,))],
+            in_specs=[hbm] * 4,
+            out_specs=[hbm] * 4,
+            scratch_shapes=[pltpu.VMEM((rank, users_dev), f32), pltpu.VMEM((rank, block), f32)] * 2 + [pltpu.SemaphoreType.DMA((2, 4))],
             compiler_params=pltpu.CompilerParams(vmem_limit_bytes=60 * 1024 * 1024),
             name="place",
         )(*outs)

time: 132 us -> 132 us (level)
  no operation moved by 1% of the time
where the time goes in v15:
time: 132 us
  Pallas kernels  131 us (99%)
    pallas_call x1, Pallas kernels, device_body(): pl.pallas_call(functools.partial(kernel, shards, step_u, step_v), out_sha...  129 us

profile of v15, /device:TPU:0, one launch (start us, length us, event | category | flops | bytes accessed | tf_op | source)
XLA Modules:
  0.0 131.8 jit_solution(8699518405006955165)
XLA Ops:
  0.6 129.4 %sweep_ring.1 = (f32[32,64]{1,0:T(8,128)}, f32[32,1024]{1,0:T(8,128)}, f32[32,64]{1,0:T(8,128)}, f32[32,1024]{1,0:T(8,128)}) custom-call(f32[64,16384]{1,0:T(8,128)} %ra.1, s32[64,16384]{1,0:T(8,128)} %ma.1, f32[32,64]{1,0:T(8,128)} %bitcast.10, f32[32,1024]{1,0:T(8,128)} %bitcast.8, f32[64,16384]{1,0:T(8,128)} %rb.1, s32[64,16384]{1,0:T(8,128)} %mb.1, ...), custom_call_target="tpu_custom_call" | custom-call | tf_op jit(solution)/shard_map/sweep_ring/pallas_call | solution.py:173
  130.1 1.7 %place.1 = (f32[32,64]{1,0:T(8,128)}, f32[32,1024]{1,0:T(8,128)}, f32[32,64]{1,0:T(8,128)}, f32[32,1024]{1,0:T(8,128)}) custom-call(f32[32,64]{1,0:T(8,128)} %get-tuple-element.12.ua, f32[32,1024]{1,0:T(8,128)} %get-tuple-element.13.va, f32[32,64]{1,0:T(8,128)} %get-tuple-element.14.ub, f32[32,1024]{1,0:T(8,128)} %get-tuple-element.15.vb), custom_call_target="tpu_custom_call" | custom-call | tf_op jit(solution)/shard_map/place/pallas_call | solution.py:196
